TPU v7x, 128 devices: a whole 4x4x4 slice. The times are simulated.
128 devices in a mesh: seq: 32 (over z, y, core), opt: 4 (over x).
Axes of the slice: x: 4, y: 4, z: 4, core: 2. Of those that a mesh axis runs over, the one named last changes fastest.
Arguments:
- layer_in: bfloat16 [4, 16384, 4096], P('opt', 'seq'), may hold values from -48 to 48, as said below
- ssm_input: bfloat16 [4, 16384, 4096], P('opt', 'seq'), may hold values from -0.119628906 to 0.119628906
- grad_out: bfloat16 [4, 16384, 4096], P('opt', 'seq'), may hold values from -0.59765625 to 0.59765625
- log_decay: float32 [4, 32, 16384], P('opt', None, 'seq'), may hold values from -1 to 0, as said below
- skip_gain: float32 [32], replicated, may hold values from 0.5 to 2
- w_bc: float32 [4096, 256], P(('seq', 'opt')), may hold values from -0.0078125 to 0.0078125
- m_code: bfloat16 [4096, 256], P(('seq', 'opt')), may hold values from -1 to 1
- m_scale: float32 [256], replicated, may hold values from 0.0001 to 0.001
- row_stat: float32 [4096], P(('seq', 'opt')), may hold values from 3e-07 to 3e-06
- col_stat: float32 [256], replicated, may hold values from 3e-07 to 3e-06
Outputs:
- grad_input: bfloat16 [4, 16384, 4096], P('opt', 'seq')
- update: float32 [4096, 256], P(('seq', 'opt'))
- code_next: bfloat16 [4096, 256], P(('seq', 'opt'))
- scale_next: float32 [256], replicated
- row_next: float32 [4096], P(('seq', 'opt'))
- col_next: float32 [256], replicated
Inputs may be any that keep to these rules, and one draw needn't show every extreme that they name: `layer_in`: real-valued rows of order one. `log_decay`: negative log decays.
All inputs are finite; a program needn't handle non-finite values.
Results may differ from a plain program's by a relative error of at most 0.0095.
Values may be sent and summed in bfloat16 or wider, within the bound.
A program may use at most 256 MiB of HBM per device.

v0:
```python
import functools

import jax
import jax.numpy as jnp
from jax import lax
from jax.sharding import Mesh
from jax.sharding import PartitionSpec as P

D = 4096
BLOCK = 256
SEQ_OPT = ("seq_0", "seq_1", "seq_2", "opt")
SEQ = ("seq_0", "seq_1", "seq_2")


beta_one = 0.9
beta_two = 0.95
weight_decay = 0.1
clip_norm = 1.0
tiny_square = 1e-30
adam_floor = 1e-08
peak_floor = 1e-06
norm_floor = 1e-06
highest = lax.Precision.HIGHEST


def filled_with(array, identity):
    return jax.tree.map(
        lambda a, e: jnp.broadcast_to(jnp.asarray(e, a.dtype), a.shape), array, identity
    )


def entering(array, axes, combine, identity, reverse):
    before = start = filled_with(array, identity)
    so_far = array
    for axis in reversed(axes):
        devices, position = (lax.axis_size(axis), lax.axis_index(axis))
        pieces = jax.tree.map(lambda part: lax.all_gather(part, axis), so_far)
        inside, so_far = (start, start)
        for k in reversed(range(devices)) if reverse else range(devices):
            passed = k > position if reverse else k < position
            so_far = combine(so_far, jax.tree.map(lambda part: part[k], pieces))
            inside = jax.tree.map(lambda new, old: jnp.where(passed, new, old), so_far, inside)
        before = combine(inside, before)
    return before


def cut_along(array, dim, devices):
    dims = array.shape
    parts = array.reshape(*dims[:dim], devices, dims[dim] // devices, *dims[dim + 1 :])
    return jnp.moveaxis(parts, dim, 0)


def sum_at_owner(array, axis, dim):
    parts = cut_along(array, dim, lax.axis_size(axis))
    arrived = lax.all_to_all(parts, axis, split_axis=0, concat_axis=0, tiled=True)
    return arrived.astype(jnp.float32).sum(axis=0)


def summed_on_arrival(array, axis, dim):
    devices = lax.axis_size(axis)
    parts = lax.all_to_all(cut_along(array, dim, devices), axis, 0, 0, tiled=True)
    return jnp.sum(parts, axis=0)


def one_axis_at_a_time(array, axes):
    return functools.reduce(lax.psum, axes, array)


def by_axis(array, axes):
    for axis in axes:
        array = lax.pmax(array, axis)
    return array


def lower_decays(running):
    length = running.shape[1]
    row_pos = lax.broadcasted_iota(jnp.int32, (length, length), 0)
    col_pos = lax.broadcasted_iota(jnp.int32, (length, length), 1)
    spread = running[:, :, None] - running[:, None, :]
    return jnp.exp(jnp.where((row_pos >= col_pos)[None], spread, -jnp.inf))


def state_adds(feat_blk, cot_blk, b_rows, c_rows, running):
    closing = running[:, -1]
    shrink = jnp.exp(closing[:, None] - running)
    grow = jnp.exp(running)
    forward_add = jnp.einsum(
        "htn,thp->hnp", shrink[:, :, None] * b_rows[None], feat_blk, precision=highest
    )
    backward_add = jnp.einsum(
        "htn,thp->hnp", grow[:, :, None] * c_rows[None], cot_blk, precision=highest
    )
    return (forward_add, backward_add)


def block_terms(halves, feat_blk, cot_blk, b_rows, c_rows, running, state_in, grad_in, skip_gain):
    feat_half, cot_half, b_half, c_half = halves
    closing = running[:, -1]
    decays = lower_decays(running)
    grow = jnp.exp(running)
    shrink = jnp.exp(closing[:, None] - running)
    intersection = jnp.einsum(
        "thp,shp->hts", feat_half, cot_half, preferred_element_type=jnp.float32
    )
    affinity = lax.dot_general(
        b_half, c_half, (((1,), (1,)), ((), ())), preferred_element_type=jnp.float32
    )
    mixing = jnp.sum(decays * jnp.transpose(intersection, (0, 2, 1)), axis=0)
    left_in = jnp.einsum("hnp,thp->htn", state_in, cot_blk, precision=highest)
    grad_cmat = jnp.dot(mixing, b_rows, precision=highest) + jnp.sum(
        grow[:, :, None] * left_in, axis=0
    )
    right_in = jnp.einsum("hnp,thp->htn", grad_in, feat_blk, precision=highest)
    grad_bmat = jnp.dot(mixing.T, c_rows, precision=highest) + jnp.sum(
        shrink[:, :, None] * right_in, axis=0
    )
    weighted = jnp.transpose(decays, (0, 2, 1)) * affinity[None]
    inner = jnp.einsum("hts,shp->thp", weighted, cot_blk, precision=highest)
    outer = jnp.einsum("tn,hnp->thp", b_rows, grad_in, precision=highest) * shrink.T[:, :, None]
    grad_feat = inner + outer + skip_gain[None, :, None] * cot_blk
    return (grad_feat, jnp.concatenate([grad_bmat, grad_cmat], axis=1))


def chain_step(earlier, later):
    return (earlier[0] * later[0], later[0][:, None, None] * earlier[1] + later[1])


def per_device(
    layer_in, ssm_input, grad_out, log_decay, skip_gain, w_bc, m_code, m_scale, row_stat, col_stat
):
    layer_rows = layer_in[0]
    length = layer_rows.shape[0]
    heads = skip_gain.shape[0]
    head_dim = ssm_input.shape[2] // heads
    state_dim = w_bc.shape[1] // 2
    w_half = w_bc.astype(jnp.bfloat16)
    columns = layer_rows
    proj = jnp.dot(
        columns,
        lax.all_gather(w_half, SEQ_OPT, axis=0, tiled=True),
        preferred_element_type=jnp.float32,
    ).astype(jnp.bfloat16)
    b_bf = proj[:, :state_dim]
    c_bf = proj[:, state_dim:]
    b_all = b_bf.astype(jnp.float32)
    c_all = c_bf.astype(jnp.float32)
    feat_bf = ssm_input[0].reshape(length, heads, head_dim)
    cot_bf = grad_out[0].reshape(length, heads, head_dim)
    feats = feat_bf.astype(jnp.float32)
    cots = cot_bf.astype(jnp.float32)
    logs = log_decay[0]
    count = length // BLOCK
    pieces = []
    halves_list = []
    for number in range(count):
        lower_end = number * BLOCK
        upper_end = lower_end + BLOCK
        running = jnp.cumsum(logs[:, lower_end:upper_end], axis=1)
        pieces.append(
            (
                feats[lower_end:upper_end],
                cots[lower_end:upper_end],
                b_all[lower_end:upper_end],
                c_all[lower_end:upper_end],
                running,
            )
        )
        halves_list.append(
            (
                feat_bf[lower_end:upper_end],
                cot_bf[lower_end:upper_end],
                b_bf[lower_end:upper_end],
                c_bf[lower_end:upper_end],
            )
        )
    zero_state = jnp.zeros((heads, state_dim, head_dim), jnp.float32)
    local_in = [zero_state]
    backward_adds = []
    start_logs = [jnp.zeros((heads,), jnp.float32)]
    for number in range(count):
        feat_blk, cot_blk, b_rows, c_rows, running = pieces[number]
        forward_add, backward_add = state_adds(feat_blk, cot_blk, b_rows, c_rows, running)
        local_in.append(jnp.exp(running[:, -1])[:, None, None] * local_in[number] + forward_add)
        backward_adds.append(backward_add)
        start_logs.append(start_logs[number] + running[:, -1])
    local_out = [zero_state] * count
    after_logs = [jnp.zeros((heads,), jnp.float32)] * count
    carried = zero_state
    after_sum = jnp.zeros((heads,), jnp.float32)
    for number in reversed(range(count)):
        local_out[number] = carried
        after_logs[number] = after_sum
        running = pieces[number][4]
        carried = jnp.exp(running[:, -1])[:, None, None] * carried + backward_adds[number]
        after_sum = after_sum + running[:, -1]
    carry_decay = jnp.exp(start_logs[count])
    identity = (jnp.ones((heads,), jnp.float32), zero_state)
    state_in = entering((carry_decay, local_in[count]), SEQ, chain_step, identity, False)[1]
    grad_in = entering((carry_decay, carried), SEQ, chain_step, identity, True)[1]
    grad_feats = []
    grad_bcs = []
    for number in range(count):
        feat_blk, cot_blk, b_rows, c_rows, running = pieces[number]
        block_state = local_in[number] + jnp.exp(start_logs[number])[:, None, None] * state_in
        block_grad = local_out[number] + jnp.exp(after_logs[number])[:, None, None] * grad_in
        grad_feat, grad_bc = block_terms(
            halves_list[number],
            feat_blk,
            cot_blk,
            b_rows,
            c_rows,
            running,
            block_state,
            block_grad,
            skip_gain,
        )
        grad_feats.append(grad_feat)
        grad_bcs.append(grad_bc)
    grad_input = (
        jnp.concatenate(grad_feats, axis=0)
        .reshape(length, heads * head_dim)
        .astype(jnp.bfloat16)[None]
    )
    grad_bc_all = jnp.concatenate(grad_bcs, axis=0).astype(jnp.bfloat16)
    columns = layer_rows
    partial_sum = sum_at_owner(
        lax.dot_general(
            columns, grad_bc_all, (((0,), (0,)), ((), ())), preferred_element_type=jnp.float32
        ).astype(jnp.bfloat16),
        SEQ,
        0,
    )
    grad_sum = summed_on_arrival(partial_sum, "opt", 0)
    col_raw, old_total = (
        one_axis_at_a_time(jnp.sum(grad_sum * grad_sum, axis=0), SEQ_OPT),
        one_axis_at_a_time(jnp.sum(row_stat), SEQ_OPT),
    )
    raw_total = jnp.sum(col_raw)
    factor = jnp.minimum(1.0, clip_norm / jnp.sqrt(raw_total + norm_floor))
    scaled = grad_sum * factor
    squares = scaled * scaled
    col_next = beta_two * col_stat + (1.0 - beta_two) * (
        factor * factor * col_raw / D + tiny_square
    )
    row_next = beta_two * row_stat + (1.0 - beta_two) * (jnp.mean(squares, axis=1) + tiny_square)
    row_mean = (
        beta_two * old_total
        + (1.0 - beta_two) * (factor * factor * raw_total / (2 * state_dim) + D * tiny_square)
    ) / D
    moment = beta_one * m_code.astype(jnp.float32) * m_scale[None, :] + (1.0 - beta_one) * scaled
    second = row_next[:, None] * col_next[None, :] / row_mean
    update = moment / (jnp.sqrt(second) + adam_floor) + weight_decay * w_bc
    col_peak = by_axis(jnp.max(jnp.abs(moment), axis=0), SEQ_OPT)
    scale_next = col_peak + peak_floor
    code_next = (moment / scale_next[None, :]).astype(jnp.bfloat16)
    return (grad_input, update, code_next, scale_next, row_next, col_next)


def solution(mesh):
    finer = Mesh(
        mesh.devices.reshape(4, 4, 2, mesh.shape["opt"]), ("seq_0", "seq_1", "seq_2", "opt")
    )
    return jax.shard_map(
        per_device,
        mesh=finer,
        in_specs=(
            P("opt", SEQ, None),
            P("opt", SEQ, None),
            P("opt", SEQ, None),
            P("opt", None, SEQ),
            P(),
            P(SEQ_OPT, None),
            P(SEQ_OPT, None),
            P(),
            P(SEQ_OPT),
            P(),
        ),
        out_specs=(P("opt", SEQ, None), P(SEQ_OPT, None), P(SEQ_OPT, None), P(), P(SEQ_OPT), P()),
        check_vma=False,
    )
```

profile of v0, /device:TPU:1, one launch (start us, length us, event | category | flops | bytes accessed | tf_op | source)
XLA Modules:
  0.0 626.6 jit_solution(1095380999536055391)
XLA Ops:
  11.0 6.4 %copy.129 = bf16[1,512,4096]{1,2,0:T(8,128)(2,1)} copy(bf16[1,512,4096]{2,1,0:T(8,128)(2,1)} %param.12) | data formatting | bytes 8388608 | tf_op args[2]
  18.1 3.8 fusion.120
  21.9 58.7 %all-gather.14.cloned.1.call-done = bf16[4096,256]{1,0:T(8,128)(2,1)} async-done(((bf16[32,256]{1,0:T(8,128)(2,1)}), bf16[4096,256]{1,0:T(8,128)(2,1)}) %all-gather.14.cloned.1.call-update) | async-done | bytes 2097168 | tf_op jit(solution)/shard_map/all_gather | solution.py:140
  80.5 4.1 fusion.75
  85.0 2.3 fusion.26
  88.6 3.6 multiply_add_fusion.4
  92.5 4.7 fusion.118
  97.1 3.4 copy.176
  100.6 4.8 copy.177
  105.6 2.3 fusion.19
  109.2 3.6 multiply_add_fusion.1
  116.2 2.5 all-reduce
  118.8 6.2 all-reduce.1
  125.1 3.9 bitcast_add_fusion.12
  129.1 3.9 bitcast_add_fusion.6
  133.7 78.1 %all-gather.16.cloned.1.call-done = f32[4,32,128,128]{3,2,1,0:T(8,128)} async-done(((f32[1,32,128,128]{3,2,1,0:T(8,128)}), f32[4,32,128,128]{3,2,1,0:T(8,128)}) %all-gather.16.cloned.1.call-update) | async-done | bytes 8388624 | tf_op jit(solution)/shard_map/all_gather | solution.py:37
  211.8 85.6 %all-gather.20.cloned.1.call-done = f32[4,32,128,128]{3,2,1,0:T(8,128)} async-done(((f32[1,32,128,128]{3,2,1,0:T(8,128)}), f32[4,32,128,128]{3,2,1,0:T(8,128)}) %all-gather.20.cloned.1.call-update) | async-done | bytes 8388624 | tf_op jit(solution)/shard_map/all_gather | solution.py:37
  297.3 8.5 %multiply_add_fusion = (f32[1,32,128,128]{3,2,1,0:T(8,128)}, f32[1,32,128,128]{3,2,1,0:T(8,128)}) fusion(f32[4,32,128,128]{3,2,1,0:T(8,128)} %all-gather.20.cloned.1.call-done, f32[32]{0:T(128)S(1)} %get-tuple-element.84, f32[32]{0:T(128)S(1)} %get-tuple-element.86, f32[32]{0:T(128)S(1)} %get-tuple-element.91, f32[32]{0:T(128)S(1)} %get-tuple-element.85, ...), kind=kLoop, calls=%fused_computation.91 | loop fusion | flops 7340032 | bytes 20972288 | tf_op jit(solution)/shard_map/add | solution.py:125
  307.3 6.2 fusion.119
  313.5 5.6 copy.139
  319.2 5.8 copy.141
  325.1 8.9 %all-gather.4 = f32[4,1,32]{2,1,0:T(1,128)S(1)} all-gather(f32[1,1,32]{2,1,0:T(1,128)S(1)} %get-tuple-element.78), channel_id=1, replica_groups=mesh['seq_0'=4,'seq_1'=4,'seq_2'=2,'opt'=4] {'seq_0'}, dimensions={0}, use_global_device_ids=true | all-gather | bytes 640 | tf_op jit(solution)/shard_map/all_gather | solution.py:37
  334.0 6.5 %all-gather.5 = f32[4,1,32]{2,1,0:T(1,128)S(1)} all-gather(f32[1,1,32]{2,1,0:T(1,128)S(1)} %get-tuple-element.77), channel_id=1, replica_groups=mesh['seq_0'=4,'seq_1'=4,'seq_2'=2,'opt'=4] {'seq_0'}, dimensions={0}, use_global_device_ids=true | all-gather | bytes 640 | tf_op jit(solution)/shard_map/all_gather | solution.py:37
  341.8 4.1 multiply_reduce_fusion.1
  346.0 3.0 multiply_reduce_fusion
  349.2 41.2 %all-gather.22.cloned.1.call-done = f32[4,32,128,128]{3,2,1,0:T(8,128)} async-done(((f32[1,32,128,128]{3,2,1,0:T(8,128)}), f32[4,32,128,128]{3,2,1,0:T(8,128)}) %all-gather.22.cloned.1.call-update) | async-done | bytes 8388624 | tf_op jit(solution)/shard_map/all_gather | solution.py:37
  390.3 9.8 %fusion.38 = f32[32,128,128]{2,1,0:T(8,128)S(1)} fusion(f32[4,32,128,128]{3,2,1,0:T(8,128)} %all-gather.22.cloned.1.call-done, f32[4,32,128,128]{3,2,1,0:T(8,128)} %all-gather.20.cloned.1.call-done, f32[64,128,128]{2,1,0:T(8,128)} %all-gather.26.cloned.1.call-done, f32[32]{0:T(128)S(1)} %get-tuple-element.80, f32[32]{0:T(128)S(1)} %get-tuple-element.81, ...), kind=kLoop, calls=%fused_computation.51 | loop fusion | flops 16252928 | bytes 23070218 | tf_op jit(solution)/shard_map/add | solution.py:125
  404.9 71.2 %all-gather.18.cloned.1.call-done = f32[4,32,128,128]{3,2,1,0:T(8,128)} async-done(((f32[1,32,128,128]{3,2,1,0:T(8,128)}), f32[4,32,128,128]{3,2,1,0:T(8,128)}) %all-gather.18.cloned.1.call-update) | async-done | bytes 8388624 | tf_op jit(solution)/shard_map/all_gather | solution.py:37
  476.1 10.3 %fusion.45 = f32[32,128,128]{2,1,0:T(8,128)S(1)} fusion(f32[4,32,128,128]{3,2,1,0:T(8,128)} %all-gather.18.cloned.1.call-done, f32[4,32,128,128]{3,2,1,0:T(8,128)} %all-gather.16.cloned.1.call-done, f32[64,128,128]{2,1,0:T(8,128)} %all-gather.24.cloned.1.call-done, f32[32]{0:T(128)} %copy-done.28, f32[32]{0:T(128)} %copy-done.29, f32[32]{0:T(128)} %copy-done.27, ...), kind=kLoop, calls=%fused_computation.62 | loop fusion | flops 16252928 | bytes 23070218 | tf_op jit(solution)/shard_map/add | solution.py:125
  486.5 2.4 multiply_reduce_fusion.5
  495.2 8.0 %all-to-all-start = ((bf16[32,128,256]{1,2,0:T(8,128)(2,1)}), bf16[32,128,256]{1,2,0:T(8,128)(2,1)}, u32[]{:S(2)}, u32[]{:S(2)}) async-start(bf16[32,128,256]{1,2,0:T(8,128)(2,1)} %bitcast.287), calls=%async_computation | async-start | bytes 4194304 | tf_op jit(solution)/shard_map/all_to_all | solution.py:55
  503.2 7.2 %fusion.5 = f32[32,256,128]{2,1,0:T(8,128)S(1)} fusion(bf16[256,32,128]{0,2,1:T(8,128)(2,1)} %bitcast.281, f32[256,256]{1,0:T(8,128)S(1)} %fusion.97, f32[32,256]{1,0:T(8,128)S(1)} %copy-done.21, pred[256,256]{1,0:T(8,128)(4,1)S(1)} %copy-done.23), kind=kOutput, calls=%fused_computation.7 | convolution fusion | flops 3227516928 | bytes 6651904 | tf_op jit(solution)/shard_map/hts,shp->thp/dot_general | solution.py:118
  510.7 5.5 fusion
  516.3 4.2 fusion.11
  520.5 4.7 fusion.13
  525.2 6.5 %all-to-all-done = bf16[32,128,256]{1,2,0:T(8,128)(2,1)} async-done(((bf16[32,128,256]{1,2,0:T(8,128)(2,1)}), bf16[32,128,256]{1,2,0:T(8,128)(2,1)}, u32[]{:S(2)}, u32[]{:S(2)}) %all-to-all-start) | async-done | bytes 2097184 | tf_op jit(solution)/shard_map/all_to_all | solution.py:55
  534.3 4.0 all-to-all-start.1
  538.3 4.0 pad_maximum_fusion
  542.2 6.5 %copy.142 = bf16[512,32,128]{0,2,1:T(8,128)(2,1)} copy(bf16[512,32,128]{2,0,1:T(8,128)(2,1)} %pad_maximum_fusion) | data formatting | bytes 8388608 | tf_op jit(solution)/shard_map/concatenate | solution.py:220
  548.8 6.3 %copy.160 = bf16[1,512,4096]{2,1,0:T(8,128)(2,1)} copy(bf16[1,512,4096]{1,2,0:T(8,128)(2,1)} %bitcast.284) | data formatting | bytes 8388608
  555.1 6.6 %all-reduce.4 = (f32[]{:T(128)}, f32[256]{0:T(256)S(1)}) all-reduce(f32[]{:T(128)} %reduce_sum.131, f32[256]{0:T(256)S(1)} %multiply_reduce_fusion.7), channel_id=1, replica_groups=mesh['seq_0'=4,'seq_1'=4,'seq_2'=2,'opt'=4] {'seq_0'}, use_global_device_ids=true, to_apply=%region_20.21 | all-reduce | flops 257 | bytes 2056 | tf_op jit(solution)/shard_map/psum | solution.py:66
  561.7 10.2 %all-reduce.3 = (f32[]{:T(128)}, f32[256]{0:T(256)S(1)}) all-reduce(f32[]{:T(128)} %get-tuple-element.39, f32[256]{0:T(256)S(1)} %get-tuple-element.40), channel_id=1, replica_groups=mesh['seq_0'=4,'seq_1'=4,'seq_2'=2,'opt'=4] {'seq_1'}, use_global_device_ids=true, to_apply=%region_21.22 | all-reduce | flops 257 | bytes 2056 | tf_op jit(solution)/shard_map/psum | solution.py:66
  571.9 5.7 all-reduce.5
  577.6 9.6 %all-reduce.2 = (f32[]{:T(128)}, f32[256]{0:T(256)S(1)}) all-reduce(f32[]{:T(128)} %get-tuple-element.41, f32[256]{0:T(256)S(1)} %get-tuple-element.42), channel_id=1, replica_groups=mesh['seq_0'=4,'seq_1'=4,'seq_2'=2,'opt'=4] {'opt'}, use_global_device_ids=true, to_apply=%region_23.24 | all-reduce | flops 257 | bytes 2056 | tf_op jit(solution)/shard_map/psum | solution.py:66
  589.3 6.6 %pmax.28 = f32[256]{0:T(256)S(1)} all-reduce(f32[256]{0:T(256)S(1)} %get-tuple-element.30), channel_id=1, replica_groups=mesh['seq_0'=4,'seq_1'=4,'seq_2'=2,'opt'=4] {'seq_0'}, use_global_device_ids=true, to_apply=%region_25.26 | all-reduce | flops 256 | bytes 2048 | tf_op jit(solution)/shard_map/pmax | solution.py:71
  595.9 7.7 %pmax.29 = f32[256]{0:T(256)S(1)} all-reduce(f32[256]{0:T(256)S(1)} %pmax.28), channel_id=1, replica_groups=mesh['seq_0'=4,'seq_1'=4,'seq_2'=2,'opt'=4] {'seq_1'}, use_global_device_ids=true, to_apply=%region_26.27 | all-reduce | flops 256 | bytes 2048 | tf_op jit(solution)/shard_map/pmax | solution.py:71
  603.6 8.5 %pmax.30 = f32[256]{0:T(256)S(1)} all-reduce(f32[256]{0:T(256)S(1)} %pmax.29), channel_id=1, replica_groups=mesh['seq_0'=4,'seq_1'=4,'seq_2'=2,'opt'=4] {'seq_2'}, use_global_device_ids=true, to_apply=%region_27.28 | all-reduce | flops 256 | bytes 2048 | tf_op jit(solution)/shard_map/pmax | solution.py:71
  612.1 6.1 pmax.31
  (167 shorter events, 29.0 us)
Async XLA Ops:
  7.2 73.4 %all-gather.14.cloned.1.call-start = ((), (), s32[]{:S(2)}) async-start(), calls=%async_computation.2 | async-start | bytes 2113536 | tf_op jit(solution)/shard_map/all_gather | solution.py:140
  8.6 116.5 %all-gather.24.cloned.1.call-start = ((), (), s32[]{:S(2)}) async-start(), calls=%async_computation.7 | async-start | bytes 6291456 | tf_op jit(solution)/shard_map/all_gather | solution.py:37
  17.6 324.2 %copy-start.20 = (f32[32,256]{1,0:T(8,128)}, f32[32,256]{1,0:T(8,128)S(1)}, u32[]{:S(2)}) copy-start(f32[32,256]{1,0:T(8,128)S(1)} %copy_bitcast_fusion.2) | copy-start | bytes 98308
  17.8 69.4 %copy-start.24 = (f32[32]{0:T(128)}, f32[32]{0:T(128)S(1)}, u32[]{:S(2)}) copy-start(f32[32]{0:T(128)S(1)} %get-tuple-element.90) | copy-start | bytes 388
  17.9 69.4 %copy-start.35 = (f32[32]{0:T(128)}, f32[32]{0:T(128)S(1)}, u32[]{:S(2)}) copy-start(f32[32]{0:T(128)S(1)} %get-tuple-element.88) | copy-start | bytes 388
  17.9 90.0 %copy-start.33 = (f32[32]{0:T(128)}, f32[32]{0:T(128)S(1)}, u32[]{:S(2)}) copy-start(f32[32]{0:T(128)S(1)} %get-tuple-element.87) | copy-start | bytes 388
  21.9 63.1 %copy-start.10 = (bf16[1,256,4096]{1,2,0:T(8,128)(2,1)}, bf16[1,256,4096]{1,2,0:T(8,128)(2,1)S(1)}, u32[]{:S(2)}) copy-start(bf16[1,256,4096]{1,2,0:T(8,128)(2,1)S(1)} %get-tuple-element.52) | copy-start | bytes 6291460
  84.9 3.6 copy-start.14
  92.2 36.9 %all-gather.26.cloned.1.call-start = ((), (), s32[]{:S(2)}) async-start(), calls=%async_computation.8 | async-start | bytes 6291456 | tf_op jit(solution)/shard_map/all_gather | solution.py:37
  100.6 241.2 %copy-start.3 = (bf16[1,256,4096]{1,2,0:T(8,128)(2,1)}, bf16[1,256,4096]{1,2,0:T(8,128)(2,1)S(1)}, u32[]{:S(2)}) copy-start(bf16[1,256,4096]{1,2,0:T(8,128)(2,1)S(1)} %copy.176) | copy-start | bytes 6291460
  105.6 3.6 copy-start.5
  112.8 98.9 %all-gather.16.cloned.1.call-start = ((), (), s32[]{:S(2)}) async-start(), calls=%async_computation.3 | async-start | bytes 10485760 | tf_op jit(solution)/shard_map/all_gather | solution.py:37
  125.1 3.9 copy-start.28
  125.1 3.9 copy-start.29
  125.1 172.2 %copy-start.27 = (f32[32]{0:T(128)}, f32[32]{0:T(128)S(1)}, u32[]{:S(2)}) copy-start(f32[32]{0:T(128)S(1)} %get-tuple-element.83) | copy-start | bytes 388
  129.0 168.3 %all-gather.20.cloned.1.call-start = ((), (), s32[]{:S(2)}) async-start(), calls=%async_computation.5 | async-start | bytes 10485760 | tf_op jit(solution)/shard_map/all_gather | solution.py:37
  133.0 257.3 %all-gather.22.cloned.1.call-start = ((), (), s32[]{:S(2)}) async-start(), calls=%async_computation.6 | async-start | bytes 10485760 | tf_op jit(solution)/shard_map/all_gather | solution.py:37
  133.7 172.2 %copy-start.26 = (f32[32]{0:T(128)}, f32[32]{0:T(128)S(1)}, u32[]{:S(2)}) copy-start(f32[32]{0:T(128)S(1)} %get-tuple-element.92) | copy-start | bytes 388
  305.9 170.2 %all-gather.18.cloned.1.call-start = ((), (), s32[]{:S(2)}) async-start(), calls=%async_computation.4 | async-start | bytes 10485760 | tf_op jit(solution)/shard_map/all_gather | solution.py:37
  319.2 22.1 %copy-start.38 = (f32[256]{0:T(256)S(1)}, f32[256]{0:T(256)}, u32[]{:S(2)}) copy-start(f32[256]{0:T(256)} %param.17) | copy-start | bytes 3076
  341.8 4.1 copy-start.6
  341.8 4.1 copy-start.11
  390.3 9.8 %copy-start.15 = (bf16[1,256,4096]{1,2,0:T(8,128)(2,1)S(1)}, bf16[1,256,4096]{1,2,0:T(8,128)(2,1)}, u32[]{:S(2)}) copy-start(bf16[1,256,4096]{1,2,0:T(8,128)(2,1)} %get-tuple-element.51) | copy-start | bytes 6291460
  400.2 2.2 copy-start.9
  400.2 2.5 copy-start.12
  400.2 2.5 copy-start.34
  400.2 2.5 copy-start.36
  476.1 10.4 %copy-start.1 = (f32[32,128,128]{2,1,0:T(8,128)S(1)}, f32[32,128,128]{2,1,0:T(8,128)}, u32[]{:S(2)}) copy-start(f32[32,128,128]{2,1,0:T(8,128)} %copy-done) | copy-start | bytes 6291460
  476.1 10.4 %copy-start.4 = (bf16[1,256,4096]{1,2,0:T(8,128)(2,1)S(1)}, bf16[1,256,4096]{1,2,0:T(8,128)(2,1)}, u32[]{:S(2)}) copy-start(bf16[1,256,4096]{1,2,0:T(8,128)(2,1)} %copy-done.3) | copy-start | bytes 6291460
  476.1 10.4 %copy-start.25 = (f32[32]{0:T(128)S(1)}, f32[32]{0:T(128)}, u32[]{:S(2)}) copy-start(f32[32]{0:T(128)} %copy-done.24) | copy-start | bytes 388
  486.5 2.4 copy-start.7
  488.9 3.2 copy-start.40
  495.2 8.0 %copy-start.21 = (f32[32,256]{1,0:T(8,128)S(1)}, f32[32,256]{1,0:T(8,128)}, u32[]{:S(2)}) copy-start(f32[32,256]{1,0:T(8,128)} %copy-done.20) | copy-start | bytes 98308
  495.2 8.0 %copy-start.23 = (pred[256,256]{1,0:T(8,128)(4,1)S(1)}, pred[256,256]{1,0:T(8,128)(4,1)}, u32[]{:S(2)}) copy-start(pred[256,256]{1,0:T(8,128)(4,1)} %iota_compare_fusion.1) | copy-start | bytes 196612
  495.2 36.4 %all-to-all-start = ((bf16[32,128,256]{1,2,0:T(8,128)(2,1)}), bf16[32,128,256]{1,2,0:T(8,128)(2,1)}, u32[]{:S(2)}, u32[]{:S(2)}) async-start(bf16[32,128,256]{1,2,0:T(8,128)(2,1)} %bitcast.287), calls=%async_computation | async-start | bytes 4194304 | tf_op jit(solution)/shard_map/all_to_all | solution.py:55
  503.2 7.5 %copy-start.13 = (bf16[1,256,4096]{1,2,0:T(8,128)(2,1)S(1)}, bf16[1,256,4096]{1,2,0:T(8,128)(2,1)}, u32[]{:S(2)}) copy-start(bf16[1,256,4096]{1,2,0:T(8,128)(2,1)} %copy-done.10) | copy-start | bytes 6291460
  510.7 5.6 copy-start.17
  510.7 5.6 copy-start.32
  516.3 4.2 copy-start.2
  516.3 4.2 copy-start.16
  525.2 13.1 %copy-start.18 = (bf16[256,32,128]{2,0,1:T(8,128)(2,1)S(1)}, bf16[256,32,128]{2,0,1:T(8,128)(2,1)}, u32[]{:S(2)}) copy-start(bf16[256,32,128]{2,0,1:T(8,128)(2,1)} %fusion.11) | copy-start | bytes 6291460
  534.3 14.4 %all-to-all-start.1 = ((f32[4,32,256]{2,1,0:T(8,128)}), f32[4,32,256]{2,1,0:T(8,128)S(1)}, u32[]{:S(2)}, u32[]{:S(2)}) async-start(f32[4,32,256]{2,1,0:T(8,128)} %bitcast.56), calls=%async_computation.1 | async-start | bytes 262144 | tf_op jit(solution)/shard_map/all_to_all | solution.py:61
  548.7 40.4 %copy-start.37 = (f32[256]{0:T(256)S(1)}, f32[256]{0:T(256)}, u32[]{:S(2)}) copy-start(f32[256]{0:T(256)} %param.19) | copy-start | bytes 3076
  548.8 40.4 %copy-start.22 = (bf16[32,256]{1,0:T(8,128)(2,1)S(1)}, bf16[32,256]{1,0:T(8,128)(2,1)}, u32[]{:S(2)}) copy-start(bf16[32,256]{1,0:T(8,128)(2,1)} %param.16) | copy-start | bytes 49156
  548.8 69.4 %copy-start.42 = (f32[32]{0:T(128)S(1)}, f32[32]{0:T(128)}, u32[]{:S(2)}) copy-start(f32[32]{0:T(128)} %param.18) | copy-start | bytes 388
  548.8 70.1 %copy-start.19 = (f32[32,256]{1,0:T(8,128)S(1)}, f32[32,256]{1,0:T(8,128)}, u32[]{:S(2)}) copy-start(f32[32,256]{1,0:T(8,128)} %param.15) | copy-start | bytes 98308
  589.1 30.5 %copy-start.30 = (f32[256]{0:T(256)}, f32[256]{0:T(256)S(1)}, u32[]{:S(2)}) copy-start(f32[256]{0:T(256)S(1)} %multiply_add_fusion.7) | copy-start | bytes 3076
  618.2 1.4 copy-start.31
  (6 other events, 6.8 us)
Sparse Core Ops, SparseCore 0:
  11.5 68.9 all-gather.13
  92.3 13.7 all-gather.23
  113.0 13.3 all-gather.25
  129.2 82.5 all-gather.15
  213.3 84.0 all-gather.19
  306.0 84.2 all-gather.21
  392.0 84.0 all-gather.17
where the time goes:
time: 635 us; the launch traced here: 627 us
  waiting for transfers between devices  342 us (54%)
  blocking collectives  85.1 us (13%)
  local copies, waits for them, and re-layouts  62.7 us (10%)
  matrix products  56.1 us (9%)
  other arithmetic  49.8 us (8%)
  between operations  18.4 us (3%)
  starting transfers between devices  12.4 us (2%)
    all_gather x6, waiting for transfers between devices, entering(): pieces = jax.tree.map(lambda part: lax.all_gather(part, axis), so_far)  276 us
    all_gather x1, waiting for transfers between devices, per_device(): lax.all_gather(w_half, SEQ_OPT, axis=0, tiled=True)  58.7 us
    add x5, other arithmetic, chain_step(): later[0][:, None, None] * earlier[1] + later[1]  36.4 us
    psum x4, blocking collectives, one_axis_at_a_time(): return functools.reduce(lax.psum, axes, array)  32 us
    pmax x4, blocking collectives, by_axis(): array = lax.pmax(array, axis)  28.9 us
    unnamed x100, local copies, waits for them, and re-layouts  26.8 us
    slice x4, local copies, waits for them, and re-layouts, per_device(): cots[lower_end:upper_end]  21.4 us
    all_gather x2, blocking collectives, entering(): pieces = jax.tree.map(lambda part: lax.all_gather(part, axis), so_far)  15.5 us
  transfers between devices with their start and end apart: 9, of which 6 were waited for; matrix products, arithmetic and copies ran while one was open for 18% of the time, Pallas kernels for 0%

commit v1 on v0

v1 whole, which is shorter than its diff:
```python
import functools

import jax
import jax.numpy as jnp
from jax import lax
from jax.experimental import pallas as pl
from jax.experimental.pallas import tpu as pltpu
from jax.sharding import PartitionSpec as P

MESH = pl.DeviceIdType.MESH
BLOCK = 256
N = 128
F32 = jnp.float32
BF16 = jnp.bfloat16
HIGH = lax.Precision.HIGHEST

beta_one = 0.9
beta_two = 0.95
weight_decay = 0.1
clip_norm = 1.0
tiny_square = 1e-30
adam_floor = 1e-08
peak_floor = 1e-06
norm_floor = 1e-06


def dot_nn(a, b, precision=None):
    return lax.dot_general(a, b, (((1,), (0,)), ((), ())), preferred_element_type=F32, precision=precision)


def dot_nt(a, b, precision=None):
    return lax.dot_general(a, b, (((1,), (1,)), ((), ())), preferred_element_type=F32, precision=precision)


def kernel(
    seqs,
    opts,
    x_hbm,
    dy_hbm,
    lay_hbm,
    logs_ref,
    skip_ref,
    w_ref,
    code_ref,
    mscale_ref,
    rowstat_ref,
    colstat_ref,
    gi_hbm,
    upd_ref,
    codeo_ref,
    scaleo_ref,
    rowo_ref,
    colo_ref,
    x_v,
    dy_v,
    lay_v,
    xs_v,
    ds_v,
    gi_v,
    w_v,
    logp_v,
    r_v,
    rt_v,
    erow_v,
    mix_v,
    aff_v,
    bc_v,
    bct_v,
    f0_v,
    k1_v,
    t_v,
    pt_v,
    cb_v,
    rb_v,
    ob_v,
    ib_v,
    xb_v,
    fin_v,
    gbt_v,
    wg_v,
    rd_v,
    rss_v,
    rsr_v,
    xo_v,
    xr_v,
    dlo_v,
    dlp_v,
    dc_v,
    a1s_v,
    a1r_v,
    a2s_v,
    a2r_v,
    m1s_v,
    m1r_v,
    m2s_v,
    m2r_v,
    in_sem,
    out_sem,
    send_sem,
    recv_sem,
    blk_sem,
    chunk_sem,
):
    heads = skip_ref.shape[0]
    chips = seqs // 2
    rows = w_ref.shape[0]
    rblk = rows * opts
    width = x_hbm.shape[1]
    dim = lay_hbm.shape[1]
    groups = 4
    per = chips // groups
    lanes_g = width // groups

    seq = lax.axis_index("seq")
    opt = lax.axis_index("opt")
    chip = seq // 2
    core = seq % 2
    mate = chip * 2 + (1 - core)
    partner = (mate, opt)

    def yz(k):
        other = (chip + k) % chips
        return other, (other * 2 + core, opt)

    def xp(k):
        other = (opt + k) % opts
        return other, (seq, other)

    def remote(src, dst, s_sem, r_sem, dev):
        return pltpu.make_async_remote_copy(
            src_ref=src, dst_ref=dst, send_sem=s_sem, recv_sem=r_sem, device_id=dev, device_id_type=MESH
        )

    def wait_bytes(ref, sem):
        pltpu.make_async_copy(ref, ref, sem).wait()

    def in_copies(g):
        lanes = pl.ds(g * lanes_g, lanes_g)
        return (
            pltpu.make_async_copy(x_hbm.at[:, lanes], x_v.at[:, lanes], in_sem.at[2 * g]),
            pltpu.make_async_copy(dy_hbm.at[:, lanes], dy_v.at[:, lanes], in_sem.at[2 * g + 1]),
        )

    lay_copy = pltpu.make_async_copy(lay_hbm, lay_v, in_sem.at[2 * groups])

    barrier = pltpu.get_barrier_semaphore()
    pl.semaphore_signal(barrier, inc=1, device_id=partner, device_id_type=MESH)
    for k in range(1, opts):
        other = (opt + k) % opts
        pl.semaphore_signal(barrier, inc=1, device_id=(seq, other), device_id_type=MESH)
        pl.semaphore_signal(barrier, inc=1, device_id=(mate, other), device_id_type=MESH)
    for k in range(1, chips):
        pl.semaphore_signal(barrier, inc=1, device_id=yz(k)[1], device_id_type=MESH)

    for g in range(groups):
        for copy in in_copies(g):
            copy.start()
    lay_copy.start()

    my_block = pl.multiple_of((chip * 2 + core) * rblk, rblk)
    my_rows = pl.multiple_of(my_block + opt * rows, rows)
    w_v[pl.ds(my_rows, rows), :] = w_ref[...].astype(BF16)

    logp_v[...] = jnp.zeros_like(logp_v)
    logp_v[0:heads, :] = logs_ref[...]
    row_i = lax.broadcasted_iota(jnp.int32, (BLOCK, BLOCK), 0)
    col_i = lax.broadcasted_iota(jnp.int32, (BLOCK, BLOCK), 1)
    upper = jnp.where(row_i <= col_i, 1.0, 0.0).astype(F32)
    lower = jnp.where(row_i >= col_i, 1.0, 0.0).astype(F32)
    for b in range(2):
        part = logp_v[:, b * BLOCK : (b + 1) * BLOCK]
        r_v[b] = dot_nn(part, upper, HIGH)
        rt_v[b * BLOCK : (b + 1) * BLOCK, :] = dot_nt(lower, part, HIGH)
    total = rt_v[BLOCK - 1 : BLOCK, :] + rt_v[2 * BLOCK - 1 : 2 * BLOCK, :]
    dlo_v[...] = jnp.broadcast_to(total, dlo_v.shape)

    pl.semaphore_wait(barrier, 1 + 2 * (opts - 1) + chips - 1)

    def w_rows(start, size):
        return w_v.at[pl.ds(start, size), :]

    for k in range(1, opts):
        remote(w_rows(my_rows, rows), w_rows(my_rows, rows), send_sem.at[0], recv_sem.at[0], xp(k)[1]).start()
    remote(dlo_v, dlp_v, send_sem.at[1], recv_sem.at[1], partner).start()

    mix_v[...] = jnp.zeros_like(mix_v)
    lane_i = lax.broadcasted_iota(jnp.int32, (2 * BLOCK, N), 1)

    def column(h):
        return jnp.sum(jnp.where(lane_i == h, rt_v[...], 0.0), axis=1, keepdims=True)

    half = BLOCK // 2
    tri_a = lax.broadcasted_iota(jnp.int32, (half, BLOCK), 1) >= lax.broadcasted_iota(jnp.int32, (half, BLOCK), 0)
    tri_b = lax.broadcasted_iota(jnp.int32, (half, half), 1) >= lax.broadcasted_iota(jnp.int32, (half, half), 0)

    def decays(rt, rs):
        top = jnp.exp(jnp.where(tri_a, rs - rt[0:half], -jnp.inf))
        bottom = jnp.exp(jnp.where(tri_b, rs[:, half:] - rt[half:], -jnp.inf))
        return top, bottom

    def mix_pair(hp, carry):
        adds = [[None, None], [None, None]]
        for j in range(2):
            h = hp * 2 + j
            lanes = pl.ds(pl.multiple_of(h * N, N), N)
            col = column(h)
            for b in range(2):
                at = pl.ds(b * BLOCK, BLOCK)
                xb = x_v[at, lanes]
                db = dy_v[at, lanes]
                rt = col[b * BLOCK : (b + 1) * BLOCK]
                rs = r_v[b, pl.ds(h, 1), :]
                prod = dot_nt(xb, db)
                top, bottom = decays(rt, rs)
                top = top * prod[0:half]
                bottom = bottom * prod[half:, half:]
                adds[b][0] = top if j == 0 else adds[b][0] + top
                adds[b][1] = bottom if j == 0 else adds[b][1] + bottom
                closing = rt[BLOCK - 1 : BLOCK]
                erow_v[b, :, lanes] = jnp.broadcast_to(jnp.exp(closing), (8, N))
                xs_v[at, lanes] = (xb.astype(F32) * jnp.exp(closing - rt)).astype(BF16)
                ds_v[at, lanes] = (db.astype(F32) * jnp.exp(rt)).astype(BF16)
        for b in range(2):
            mix_v[b, 0:half, :] += adds[b][0]
            mix_v[b, half:, half:] += adds[b][1]
        return carry

    pairs_g = heads // 2 // groups
    for g in range(groups):
        for copy in in_copies(g):
            copy.wait()
        lax.fori_loop(g * pairs_g, (g + 1) * pairs_g, mix_pair, 0)
        if g == 0:
            wait_bytes(w_rows(0, rows * (opts - 1)), recv_sem.at[0])
            for k in range(1, chips):
                remote(
                    w_rows(my_block, rblk), w_rows(my_block, rblk), send_sem.at[2], blk_sem.at[k], yz(k)[1]
                ).start()
            remote(w_rows(my_block, rblk), w_rows(my_block, rblk), send_sem.at[3], recv_sem.at[3], partner).start()
            wait_bytes(dlp_v, recv_sem.at[1])
            dc_v[chip] = dlo_v[...] + dlp_v[...]
            for k in range(1, chips):
                remote(dc_v.at[chip], dc_v.at[chip], send_sem.at[4], recv_sem.at[4], yz(k)[1]).start()

    for k in range(1, chips):
        source = (chip + chips - k) % chips
        start = pl.multiple_of((source * 2 + core) * rblk, rblk)
        wait_bytes(w_rows(start, rblk), blk_sem.at[k])
        remote(w_rows(start, rblk), w_rows(start, rblk), send_sem.at[3], recv_sem.at[3], partner).start()
    lay_copy.wait()
    wait_bytes(w_rows(0, rblk * chips), recv_sem.at[3])

    proj = dot_nn(lay_v[...], w_v[...]).astype(BF16)
    bc_v[...] = proj
    bct_v[...] = jnp.transpose(proj.astype(F32)).astype(BF16)
    for b in range(2):
        at = slice(b * BLOCK, (b + 1) * BLOCK)
        aff_v[b] = dot_nt(bc_v[at, 0:N], bc_v[at, N : 2 * N])

    def add_pair(o, carry):
        lanes = pl.ds(pl.multiple_of(o * 2 * N, 2 * N), 2 * N)
        e0 = erow_v[0, 0:1, lanes]
        e1 = erow_v[1, 0:1, lanes]
        f0 = dot_nn(bct_v[0:N, 0:BLOCK], xs_v[0:BLOCK, lanes])
        f1 = dot_nn(bct_v[0:N, BLOCK:], xs_v[BLOCK:, lanes])
        k0 = dot_nn(bct_v[N:, 0:BLOCK], ds_v[0:BLOCK, lanes])
        k1 = dot_nn(bct_v[N:, BLOCK:], ds_v[BLOCK:, lanes])
        f0_v[:, lanes] = f0
        k1_v[:, lanes] = k1
        state = (e1 * f0 + f1).astype(BF16)
        grad = (k0 + e0 * k1).astype(BF16)
        for j in range(2):
            t_v[j, o, 0] = state[:, j * N : (j + 1) * N]
            t_v[j, o, 1] = grad[:, j * N : (j + 1) * N]
        return carry

    for g in range(groups):
        lax.fori_loop(g * per, (g + 1) * per, add_pair, 0)
        piece = pl.ds(g * per, per)
        remote(t_v.at[1 - core, piece], pt_v.at[piece], send_sem.at[5], chunk_sem.at[0, g], partner).start()

    lane_r = lax.broadcasted_iota(jnp.int32, (1, N), 1)

    def decay_of(ref, h):
        return jnp.exp(jnp.sum(jnp.where(lane_r == h, ref[0:1, :], 0.0), axis=1, keepdims=True))

    first = core == 0

    def combine(o, carry):
        h = 2 * o + core
        mine = decay_of(dlo_v, h)
        theirs = decay_of(dlp_v, h)
        one = jnp.ones_like(mine)
        own_f = t_v[core, o, 0].astype(F32)
        own_b = t_v[core, o, 1].astype(F32)
        oth_f = pt_v[o, 0].astype(F32)
        oth_b = pt_v[o, 1].astype(F32)
        state = jnp.where(first, theirs, one) * own_f + jnp.where(first, one, mine) * oth_f
        grad = jnp.where(first, one, theirs) * own_b + jnp.where(first, mine, one) * oth_b
        cb_v[o, 0] = state.astype(BF16)
        cb_v[o, 1] = grad.astype(BF16)
        return carry

    for g in range(groups):
        piece = pl.ds(g * per, per)
        wait_bytes(pt_v.at[piece], chunk_sem.at[0, g])
        lax.fori_loop(g * per, (g + 1) * per, combine, 0)
    for k in range(1, chips):
        other, dev = yz(k)
        remote(cb_v.at[other], rb_v.at[chip], send_sem.at[6], recv_sem.at[6], dev).start()
    rb_v[chip] = cb_v[chip]

    def inner_pair(hp, carry):
        for j in range(2):
            h = hp * 2 + j
            lanes = pl.ds(pl.multiple_of(h * N, N), N)
            col = column(h)
            gain = skip_ref[h]
            for b in range(2):
                rt = col[b * BLOCK : (b + 1) * BLOCK]
                rs = r_v[b, pl.ds(h, 1), :]
                top, bottom = decays(rt, rs)
                top = (top * aff_v[b, 0:half, :]).astype(BF16)
                bottom = (bottom * aff_v[b, half:, half:]).astype(BF16)
                db = dy_v[pl.ds(b * BLOCK, BLOCK), lanes]
                low = db[half:]
                gi_v[pl.ds(b * BLOCK, half), lanes] = (dot_nn(top, db) + gain * db[0:half].astype(F32)).astype(BF16)
                gi_v[pl.ds(b * BLOCK + half, half), lanes] = (dot_nn(bottom, low) + gain * low.astype(F32)).astype(BF16)
        return carry

    lax.fori_loop(0, heads // 2, inner_pair, 0)

    wait_bytes(dc_v.at[pl.ds(0, chips - 1)], recv_sem.at[4])
    wait_bytes(rb_v.at[pl.ds(0, chips - 1)], recv_sem.at[6])
    lane_c = lax.broadcasted_iota(jnp.int32, (chips, N), 1)
    chip_decay = jnp.exp(jnp.sum(jnp.where(lane_c == seq, dc_v[:, 0, :], 0.0), axis=1, keepdims=True))
    run = jnp.zeros((N, N), F32)
    for o in range(chips):
        ob_v[o, 0] = run.astype(BF16)
        run = chip_decay[o : o + 1] * run + rb_v[o, 0].astype(F32)
    run = jnp.zeros((N, N), F32)
    for o in reversed(range(chips)):
        ob_v[o, 1] = run.astype(BF16)
        run = chip_decay[o : o + 1] * run + rb_v[o, 1].astype(F32)
    for k in range(1, chips):
        other, dev = yz(k)
        remote(ob_v.at[other], ib_v.at[chip], send_sem.at[7], recv_sem.at[7], dev).start()
    ib_v[chip] = ob_v[chip]

    for b in range(2):
        at = slice(b * BLOCK, (b + 1) * BLOCK)
        mix = mix_v[b].astype(BF16)
        gbt_v[0:N, at] = dot_nt(bct_v[N:, at], mix)
        gbt_v[N:, at] = dot_nn(bct_v[0:N, at], mix)

    wait_bytes(ib_v.at[pl.ds(0, chips - 1)], recv_sem.at[7])

    def entry(o, carry):
        h = 2 * o + core
        mine = decay_of(dlo_v, h)
        theirs = decay_of(dlp_v, h)
        one = jnp.ones_like(mine)
        nil = jnp.zeros_like(mine)
        state = ib_v[o, 0].astype(F32)
        grad = ib_v[o, 1].astype(F32)
        own_f = t_v[core, o, 0].astype(F32)
        own_b = t_v[core, o, 1].astype(F32)
        oth_f = pt_v[o, 0].astype(F32)
        oth_b = pt_v[o, 1].astype(F32)
        fin_v[core, o, 0] = (jnp.where(first, one, theirs) * state + jnp.where(first, nil, one) * oth_f).astype(BF16)
        fin_v[core, o, 1] = (jnp.where(first, theirs, one) * grad + jnp.where(first, one, nil) * oth_b).astype(BF16)
        xb_v[o, 0] = (jnp.where(first, mine, one) * state + jnp.where(first, one, nil) * own_f).astype(BF16)
        xb_v[o, 1] = (jnp.where(first, one, mine) * grad + jnp.where(first, nil, one) * own_b).astype(BF16)
        return carry

    for g in range(groups):
        lax.fori_loop(g * per, (g + 1) * per, entry, 0)
        piece = pl.ds(g * per, per)
        remote(xb_v.at[piece], fin_v.at[core, piece], send_sem.at[8], chunk_sem.at[1, g], partner).start()

    def finish_pair(o, carry):
        lanes = pl.ds(pl.multiple_of(o * 2 * N, 2 * N), 2 * N)
        e0 = erow_v[0, 0:1, lanes]
        e1 = erow_v[1, 0:1, lanes]
        s0 = jnp.concatenate([fin_v[0, o, 0], fin_v[1, o, 0]], axis=1)
        g1 = jnp.concatenate([fin_v[0, o, 1], fin_v[1, o, 1]], axis=1)
        s1 = (f0_v[:, lanes] + e0 * s0.astype(F32)).astype(BF16)
        g0 = (k1_v[:, lanes] + e1 * g1.astype(F32)).astype(BF16)
        cols = [column(2 * o), column(2 * o + 1)]
        for b, (st, gr) in enumerate(((s0, g0), (s1, g1))):
            at = slice(b * BLOCK, (b + 1) * BLOCK)
            gbt_v[0:N, at] += dot_nt(gr, xs_v[at, lanes])
            gbt_v[N:, at] += dot_nt(st, ds_v[at, lanes])
            outer = dot_nn(bc_v[at, 0:N], gr)
            for j in range(2):
                sub = pl.ds(pl.multiple_of((o * 2 + j) * N, N), N)
                rt = cols[j][at]
                shrink = jnp.exp(rt[BLOCK - 1 : BLOCK] - rt)
                gi_v[at, sub] = (gi_v[at, sub].astype(F32) + shrink * outer[:, j * N : (j + 1) * N]).astype(BF16)
        return carry

    def out_copy(g):
        lanes = pl.ds(g * lanes_g, lanes_g)
        return pltpu.make_async_copy(gi_v.at[:, lanes], gi_hbm.at[:, lanes], out_sem.at[g])

    for g in range(groups):
        piece = pl.ds(g * per, per)
        wait_bytes(xb_v.at[piece], chunk_sem.at[1, g])
        lax.fori_loop(g * per, (g + 1) * per, finish_pair, 0)
        out_copy(g).start()

    gbt_b = gbt_v[...].astype(BF16)

    def weight_pair(o, carry):
        lanes = pl.ds(pl.multiple_of(o * 2 * rblk, 2 * rblk), 2 * rblk)
        part = dot_nn(gbt_b, lay_v[:, lanes]).astype(BF16)
        wg_v[0, o] = part[:, 0:rblk]
        wg_v[1, o] = part[:, rblk:]
        return carry

    for g in range(groups):
        lax.fori_loop(g * per, (g + 1) * per, weight_pair, 0)
        piece = pl.ds(g * per, per)
        remote(wg_v.at[1 - core, piece], rd_v.at[piece], send_sem.at[9], chunk_sem.at[2, g], partner).start()

    def chip_sum(o, carry):
        rss_v[o] = (wg_v[core, o].astype(F32) + rd_v[o].astype(F32)).astype(BF16)
        return carry

    for g in range(groups):
        piece = pl.ds(g * per, per)
        wait_bytes(rd_v.at[piece], chunk_sem.at[2, g])
        lax.fori_loop(g * per, (g + 1) * per, chip_sum, 0)
    for k in range(1, chips):
        other, dev = yz(k)
        remote(rss_v.at[other], rsr_v.at[chip], send_sem.at[10], recv_sem.at[10], dev).start()
    rsr_v[chip] = rss_v[chip]
    wait_bytes(rsr_v.at[pl.ds(0, chips - 1)], recv_sem.at[10])
    acc = rsr_v[0].astype(F32)
    for o in range(1, chips):
        acc = acc + rsr_v[o].astype(F32)
    turned = jnp.transpose(acc)
    for k in range(opts):
        xo_v[k] = turned[k * rows : (k + 1) * rows]
    for k in range(1, opts):
        other, dev = xp(k)
        remote(xo_v.at[other], xr_v.at[opt], send_sem.at[11], recv_sem.at[11], dev).start()
    xr_v[opt] = xo_v[opt]
    wait_bytes(xr_v.at[pl.ds(0, opts - 1)], recv_sem.at[11])
    grad = xr_v[0]
    for k in range(1, opts):
        grad = grad + xr_v[k]

    near = 2 * opts

    def over_all(s1, r1, s2, r2, base, combine_fn):
        me = core * opts + opt
        r1[me] = s1[...]
        for k in range(1, near):
            other = (me + k) % near
            dev = (chip * 2 + other // opts, other % opts)
            remote(s1, r1.at[me], send_sem.at[base], recv_sem.at[base], dev).start()
        wait_bytes(r1.at[pl.ds(0, near - 1)], recv_sem.at[base])
        value = r1[0]
        for k in range(1, near):
            value = combine_fn(value, r1[k])
        s2[...] = value
        r2[chip] = value
        for k in range(1, chips):
            remote(s2, r2.at[chip], send_sem.at[base + 1], recv_sem.at[base + 1], yz(k)[1]).start()
        wait_bytes(r2.at[pl.ds(0, chips - 1)], recv_sem.at[base + 1])
        value = r2[0]
        for k in range(1, chips):
            value = combine_fn(value, r2[k])
        return value

    old_row = rowstat_ref[...]
    a1s_v[0:1, :] = jnp.sum(grad * grad, axis=0, keepdims=True)
    a1s_v[1:8, :] = jnp.broadcast_to(jnp.sum(old_row, axis=1, keepdims=True), (7, 2 * N))
    sums = over_all(a1s_v, a1r_v, a2s_v, a2r_v, 12, jnp.add)
    col_raw = sums[0:1, :]
    old_total = sums[1:2, 0:1]
    raw_total = jnp.sum(col_raw, axis=1, keepdims=True)
    factor = jnp.minimum(1.0, clip_norm / jnp.sqrt(raw_total + norm_floor))
    scaled = grad * factor
    moment = beta_one * code_ref[...].astype(F32) * mscale_ref[...] + (1.0 - beta_one) * scaled
    m1s_v[...] = jnp.broadcast_to(jnp.max(jnp.abs(moment), axis=0, keepdims=True), m1s_v.shape)
    peak = over_all(m1s_v, m1r_v, m2s_v, m2r_v, 14, jnp.maximum)[0:1, :]

    squares = scaled * scaled
    col_next = beta_two * colstat_ref[...] + (1.0 - beta_two) * (factor * factor * col_raw / dim + tiny_square)
    eye = lax.broadcasted_iota(jnp.int32, (rows, rows), 0) == lax.broadcasted_iota(jnp.int32, (rows, rows), 1)
    old_col = jnp.sum(jnp.where(eye, jnp.broadcast_to(old_row, (rows, rows)), 0.0), axis=1, keepdims=True)
    row_next = beta_two * old_col + (1.0 - beta_two) * (
        jnp.sum(squares, axis=1, keepdims=True) / (2 * N) + tiny_square
    )
    row_mean = (
        beta_two * old_total + (1.0 - beta_two) * (factor * factor * raw_total / (2 * N) + dim * tiny_square)
    ) / dim
    second = row_next * col_next / row_mean
    upd_ref[...] = moment / (jnp.sqrt(second) + adam_floor) + weight_decay * w_ref[...]
    scale_next = peak + peak_floor
    scaleo_ref[...] = scale_next
    codeo_ref[...] = (moment / scale_next).astype(BF16)
    colo_ref[...] = col_next
    rowo_ref[...] = jnp.sum(jnp.where(eye, jnp.broadcast_to(row_next, (rows, rows)), 0.0), axis=0, keepdims=True)

    for g in range(groups):
        out_copy(g).wait()
    wait_bytes(w_rows(0, rows * (opts - 1)), send_sem.at[0])
    wait_bytes(dlo_v, send_sem.at[1])
    wait_bytes(w_rows(0, rblk * (chips - 1)), send_sem.at[2])
    wait_bytes(w_rows(0, rblk * chips), send_sem.at[3])
    wait_bytes(dc_v.at[pl.ds(0, chips - 1)], send_sem.at[4])
    wait_bytes(pt_v, send_sem.at[5])
    wait_bytes(cb_v.at[pl.ds(0, chips - 1)], send_sem.at[6])
    wait_bytes(ob_v.at[pl.ds(0, chips - 1)], send_sem.at[7])
    wait_bytes(xb_v, send_sem.at[8])
    wait_bytes(rd_v, send_sem.at[9])
    wait_bytes(rss_v.at[pl.ds(0, chips - 1)], send_sem.at[10])
    wait_bytes(xo_v.at[pl.ds(0, opts - 1)], send_sem.at[11])
    for base, r1, r2 in ((12, a1r_v, a2r_v), (14, m1r_v, m2r_v)):
        wait_bytes(r1.at[pl.ds(0, near - 1)], send_sem.at[base])
        wait_bytes(r2.at[pl.ds(0, chips - 1)], send_sem.at[base + 1])


def per_device(
    seqs, opts, layer_in, ssm_input, grad_out, log_decay, skip_gain, w_bc, m_code, m_scale, row_stat, col_stat
):
    heads = skip_gain.shape[0]
    tokens, width = ssm_input.shape[1:]
    dim = layer_in.shape[2]
    rows = w_bc.shape[0]
    chips = seqs // 2
    rblk = rows * opts
    vm = pl.BlockSpec(memory_space=pltpu.VMEM)
    hbm = pl.BlockSpec(memory_space=pl.ANY)
    state = (chips, 2, N, N)
    scratch = [
        pltpu.VMEM((tokens, width), BF16),
        pltpu.VMEM((tokens, width), BF16),
        pltpu.VMEM((tokens, dim), BF16),
        pltpu.VMEM((tokens, width), BF16),
        pltpu.VMEM((tokens, width), BF16),
        pltpu.VMEM((tokens, width), BF16),
        pltpu.VMEM((dim, 2 * N), BF16),
        pltpu.VMEM((N, tokens), F32),
        pltpu.VMEM((2, N, BLOCK), F32),
        pltpu.VMEM((tokens, N), F32),
        pltpu.VMEM((2, 8, width), F32),
        pltpu.VMEM((2, BLOCK, BLOCK), F32),
        pltpu.VMEM((2, BLOCK, BLOCK), F32),
        pltpu.VMEM((tokens, 2 * N), BF16),
        pltpu.VMEM((2 * N, tokens), BF16),
        pltpu.VMEM((N, width), F32),
        pltpu.VMEM((N, width), F32),
        pltpu.VMEM((2,) + state, BF16),
        pltpu.VMEM(state, BF16),
        pltpu.VMEM(state, BF16),
        pltpu.VMEM(state, BF16),
        pltpu.VMEM(state, BF16),
        pltpu.VMEM(state, BF16),
        pltpu.VMEM(state, BF16),
        pltpu.VMEM((2,) + state, BF16),
        pltpu.VMEM((2 * N, tokens), F32),
        pltpu.VMEM((2, chips, 2 * N, rblk), BF16),
        pltpu.VMEM((chips, 2 * N, rblk), BF16),
        pltpu.VMEM((chips, 2 * N, rblk), BF16),
        pltpu.VMEM((chips, 2 * N, rblk), BF16),
        pltpu.VMEM((opts, rows, 2 * N), F32),
        pltpu.VMEM((opts, rows, 2 * N), F32),
        pltpu.VMEM((8, N), F32),
        pltpu.VMEM((8, N), F32),
        pltpu.VMEM((chips, 8, N), F32),
    ]
    for _ in range(2):
        scratch += [
            pltpu.VMEM((8, 2 * N), F32),
            pltpu.VMEM((2 * opts, 8, 2 * N), F32),
            pltpu.VMEM((8, 2 * N), F32),
            pltpu.VMEM((chips, 8, 2 * N), F32),
        ]
    scratch += [
        pltpu.SemaphoreType.DMA((9,)),
        pltpu.SemaphoreType.DMA((4,)),
        pltpu.SemaphoreType.DMA((16,)),
        pltpu.SemaphoreType.DMA((16,)),
        pltpu.SemaphoreType.DMA((chips,)),
        pltpu.SemaphoreType.DMA((3, 4)),
    ]
    out = pl.pallas_call(
        functools.partial(kernel, seqs, opts),
        out_shape=(
            jax.ShapeDtypeStruct((tokens, width), BF16),
            jax.ShapeDtypeStruct((rows, 2 * N), F32),
            jax.ShapeDtypeStruct((rows, 2 * N), BF16),
            jax.ShapeDtypeStruct((1, 2 * N), F32),
            jax.ShapeDtypeStruct((1, rows), F32),
            jax.ShapeDtypeStruct((1, 2 * N), F32),
        ),
        in_specs=[hbm, hbm, hbm, vm, pl.BlockSpec(memory_space=pltpu.SMEM), vm, vm, vm, vm, vm],
        out_specs=(hbm, vm, vm, vm, vm, vm),
        scratch_shapes=scratch,
        compiler_params=pltpu.CompilerParams(
            collective_id=0, has_side_effects=True, vmem_limit_bytes=66_000_000
        ),
    )(
        ssm_input[0],
        grad_out[0],
        layer_in[0],
        log_decay[0],
        skip_gain,
        w_bc,
        m_code,
        m_scale.reshape(1, 2 * N),
        row_stat.reshape(1, rows),
        col_stat.reshape(1, 2 * N),
    )
    grad_input, update, code_next, scale_next, row_next, col_next = out
    return (
        grad_input[None],
        update,
        code_next,
        scale_next.reshape(2 * N),
        row_next.reshape(rows),
        col_next.reshape(2 * N),
    )


def solution(mesh):
    both = ("seq", "opt")
    return jax.shard_map(
        functools.partial(per_device, mesh.shape["seq"], mesh.shape["opt"]),
        mesh=mesh,
        in_specs=(
            P("opt", "seq", None),
            P("opt", "seq", None),
            P("opt", "seq", None),
            P("opt", None, "seq"),
            P(),
            P(both, None),
            P(both, None),
            P(),
            P(both),
            P(),
        ),
        out_specs=(P("opt", "seq", None), P(both, None), P(both, None), P(), P(both), P()),
        check_vma=False,
    )
```

time: 635 us -> 128 us (0.20); the launches traced: 627 us -> 128 us
  waiting for transfers between devices: 342 us -> 0 us
  Pallas kernels: 0 us -> 119 us
  blocking collectives: 85.1 us -> 0 us
  matrix products: 56.1 us -> 0 us
  local copies, waits for them, and re-layouts: 62.7 us -> 7.58 us
  other arithmetic: 49.8 us -> 0 us
  between operations: 18.4 us -> 0.69 us
  starting transfers between devices: 12.4 us -> 0 us
    all_gather x7 -> x0, waiting for transfers between devices: 335 us -> none  [the longest x6 276 us: entering(): pieces = jax.tree.map(lambda part: lax.all_gather(part, axis), so_far)]
    pallas_call x0 -> x1, Pallas kernels: none -> 119 us  [per_device(): pl.pallas_call(functools.partial(kernel, seqs, opts), out_shape=(jax.Shap...]
    dot_general x22 -> x0, matrix products: 56.1 us -> none  [the longest x2 12.8 us: block_terms(): inner = jnp.einsum('hts,shp->thp', weighted, cot_blk, precision=highest)]
    add x8 -> x0, other arithmetic: 36.5 us -> none  [the longest x5 36.4 us: chain_step(): later[0][:, None, None] * earlier[1] + later[1]]
    psum x4 -> x0, blocking collectives: 32 us -> none  [one_axis_at_a_time(): return functools.reduce(lax.psum, axes, array)]
    pmax x4 -> x0, blocking collectives: 28.9 us -> none  [by_axis(): array = lax.pmax(array, axis)]
    slice x11 -> x0, local copies, waits for them, and re-layouts: 26.7 us -> none  [the longest x4 21.4 us: per_device(): cots[lower_end:upper_end]]
    unnamed x100 -> x16, local copies, waits for them, and re-layouts: 26.8 us -> 7.58 us
  transfers between devices with their start and end apart: 9 -> 0, of which waited for: 6 -> 0; matrix products, arithmetic and copies ran while one was open for 18% -> 0% of each run, Pallas kernels for 0% -> 0%
where the time goes in v1:
time: 128 us
  Pallas kernels  119 us (93%)
  local copies, waits for them, and re-layouts  7.58 us (6%)
    pallas_call x1, Pallas kernels, per_device(): pl.pallas_call(functools.partial(kernel, seqs, opts), out_shape=(jax.Shap...  119 us
    unnamed x16, local copies, waits for them, and re-layouts  7.58 us

profile of v1, /device:TPU:1, one launch (start us, length us, event | category | flops | bytes accessed | tf_op | source)
XLA Modules:
  0.0 127.5 jit_solution(4614178642065310426)
XLA Ops:
  0.6 119.3 %shard_map.145 = (bf16[512,4096]{1,0:T(8,128)(2,1)}, f32[32,256]{1,0:T(8,128)}, bf16[32,256]{1,0:T(8,128)(2,1)}, f32[1,256]{1,0:T(1,128)}, f32[1,32]{1,0:T(1,128)}, /*index=5*/f32[1,256]{1,0:T(1,128)}) custom-call(bf16[512,4096]{1,0:T(8,128)(2,1)} %bitcast.12, bf16[512,4096]{1,0:T(8,128)(2,1)} %bitcast.13, bf16[512,4096]{1,0:T(8,128)(2,1)} %bitcast.14, ...), custom_call_target="tpu_custom_call" | custom-call | tf_op jit(solution)/shard_map/pallas_call | solution.py:591
  119.9 0.0 copy-start
  119.9 0.0 copy-start.1
  119.9 0.0 copy-start.3
  119.9 0.0 copy-start.4
  120.0 0.0 copy-start.2
  120.0 4.7 %copy.22 = bf16[1,512,4096]{2,1,0:T(8,128)(2,1)} copy(bf16[1,512,4096]{2,1,0:T(8,128)(2,1)} %bitcast.11) | data formatting | bytes 8388608
  124.7 0.0 copy-done
  124.7 0.6 copy.23
  125.3 0.0 copy-done.1
  125.3 0.6 copy.24
  125.9 0.0 copy-done.3
  125.9 0.6 copy.25
  126.5 0.0 copy-done.4
  126.5 0.5 copy.26
  127.0 0.0 copy-done.2
  127.0 0.6 copy.27
Async XLA Ops:
  119.9 4.8 %copy-start = (f32[32,256]{1,0:T(8,128)S(1)}, f32[32,256]{1,0:T(8,128)}, u32[]{:S(2)}) copy-start(f32[32,256]{1,0:T(8,128)} %get-tuple-element.25) | copy-start | bytes 98308
  119.9 5.4 %copy-start.1 = (bf16[32,256]{1,0:T(8,128)(2,1)S(1)}, bf16[32,256]{1,0:T(8,128)(2,1)}, u32[]{:S(2)}) copy-start(bf16[32,256]{1,0:T(8,128)(2,1)} %get-tuple-element.26) | copy-start | bytes 49156
  119.9 6.0 %copy-start.3 = (f32[1,256]{1,0:T(1,128)S(1)}, f32[1,256]{1,0:T(1,128)}, u32[]{:S(2)}) copy-start(f32[1,256]{1,0:T(1,128)} %get-tuple-element.15) | copy-start | bytes 3076
  119.9 6.5 %copy-start.4 = (f32[1,32]{1,0:T(1,128)S(1)}, f32[1,32]{1,0:T(1,128)}, u32[]{:S(2)}) copy-start(f32[1,32]{1,0:T(1,128)} %get-tuple-element.16) | copy-start | bytes 388
  120.0 7.0 %copy-start.2 = (f32[1,256]{1,0:T(1,128)S(1)}, f32[1,256]{1,0:T(1,128)}, u32[]{:S(2)}) copy-start(f32[1,256]{1,0:T(1,128)} %get-tuple-element.17) | copy-start | bytes 3076

commit v2 on v1

v2 whole, which is shorter than its diff:
```python
import functools
import math

import jax
import jax.numpy as jnp
from jax import lax
from jax.experimental import pallas as pl
from jax.experimental.pallas import tpu as pltpu
from jax.sharding import PartitionSpec as P

MESH = pl.DeviceIdType.MESH
BLOCK = 256
N = 128
F32 = jnp.float32
BF16 = jnp.bfloat16
HIGH = lax.Precision.HIGHEST

beta_one = 0.9
beta_two = 0.95
weight_decay = 0.1
clip_norm = 1.0
tiny_square = 1e-30
adam_floor = 1e-08
peak_floor = 1e-06
norm_floor = 1e-06


def dot_nn(a, b, precision=None):
    return lax.dot_general(a, b, (((1,), (0,)), ((), ())), preferred_element_type=F32, precision=precision)


def dot_nt(a, b, precision=None):
    return lax.dot_general(a, b, (((1,), (1,)), ((), ())), preferred_element_type=F32, precision=precision)


def kernel(
    seqs,
    opts,
    x_hbm,
    dy_hbm,
    lay_hbm,
    logs_ref,
    skip_ref,
    w_ref,
    code_ref,
    mscale_ref,
    rowstat_ref,
    colstat_ref,
    gi_hbm,
    upd_ref,
    codeo_ref,
    scaleo_ref,
    rowo_ref,
    colo_ref,
    x_v,
    dy_v,
    lay_v,
    xs_v,
    ds_v,
    gi_v,
    w_v,
    logp_v,
    r_v,
    rt_v,
    erow_v,
    mix_v,
    aff_v,
    bc_v,
    bct_v,
    f0_v,
    k1_v,
    t_v,
    pt_v,
    cb_v,
    rb_v,
    ob_v,
    ib_v,
    xb_v,
    fin_v,
    gbt_v,
    wg_v,
    rd_v,
    rss_v,
    rsr_v,
    xg_v,
    gt_v,
    mc_v,
    rx_v,
    dlo_v,
    dlp_v,
    dc_v,
    s_v,
    m_v,
    in_sem,
    out_sem,
    send_sem,
    recv_sem,
    blk_sem,
    half_sem,
    entry_sem,
    d2d_sem,
    fin_sem,
    rs_sem,
):
    heads = skip_ref.shape[0]
    chips = seqs // 2
    rows = w_ref.shape[0]
    rblk = rows * opts
    width = x_hbm.shape[1]
    dim = lay_hbm.shape[1]
    groups = 4
    lanes_g = width // groups
    fines = min(8, chips)
    fine = chips // fines

    seq = lax.axis_index("seq")
    opt = lax.axis_index("opt")
    chip = seq // 2
    core = seq % 2
    mate = chip * 2 + (1 - core)
    partner = (mate, opt)

    side = math.isqrt(chips)

    def step_of(i):
        return (i * (i + 1) // 2) % side

    def owner_after(e):
        zs = (chip // side + step_of(e // side)) % side
        ys = (chip % side + step_of(e % side)) % side
        return zs * side + ys

    def owner_before(e):
        zs = (chip // side + side - step_of(e // side)) % side
        ys = (chip % side + side - step_of(e % side)) % side
        return zs * side + ys

    def flip(i):
        return 2 * (i % 2) + i // 2 if side == 4 else i

    def opposite(e):
        return flip(e // side) * side + flip(e % side)

    far_first = tuple(range(chips - 1, 0, -1))

    def yz(e):
        other = owner_after(e)
        return other, (other * 2 + core, opt)

    def xp(k):
        other = (opt + k) % opts
        return other, (seq, other)

    def remote(src, dst, s_sem, r_sem, dev):
        return pltpu.make_async_remote_copy(
            src_ref=src, dst_ref=dst, send_sem=s_sem, recv_sem=r_sem, device_id=dev, device_id_type=MESH
        )

    def wait_bytes(ref, sem):
        pltpu.make_async_copy(ref, ref, sem).wait()

    def in_copies(g):
        lanes = pl.ds(g * lanes_g, lanes_g)
        return (
            pltpu.make_async_copy(x_hbm.at[:, lanes], x_v.at[:, lanes], in_sem.at[2 * g]),
            pltpu.make_async_copy(dy_hbm.at[:, lanes], dy_v.at[:, lanes], in_sem.at[2 * g + 1]),
        )

    lay_copy = pltpu.make_async_copy(lay_hbm, lay_v, in_sem.at[2 * groups])

    barrier = pltpu.get_barrier_semaphore()
    for k in range(1, seqs):
        pl.semaphore_signal(barrier, inc=1, device_id=((seq + k) % seqs, opt), device_id_type=MESH)
    for k in range(1, opts):
        pl.semaphore_signal(barrier, inc=1, device_id=xp(k)[1], device_id_type=MESH)

    for g in range(groups):
        for copy in in_copies(g):
            copy.start()
    lay_copy.start()

    w_v[chip, core, opt] = w_ref[...].astype(BF16)
    mc_v[opt] = code_ref[...]
    old_row = rowstat_ref[...]
    rx_v[opt] = jnp.broadcast_to(jnp.sum(old_row, axis=1, keepdims=True), (8, N))

    left = pl.ds(0, N)
    right = pl.ds(N, N)

    def same(ref, s_sem, r_sem, dev):
        return remote(ref, ref, s_sem, r_sem, dev)

    pl.semaphore_wait(barrier, seqs - 1 + opts - 1)
    for k in range(1, opts):
        same(w_v.at[chip, core, opt, :, left], send_sem.at[0], recv_sem.at[0], xp(k)[1]).start()
    for k in far_first:
        same(w_v.at[chip, core, opt, :, right], send_sem.at[12], recv_sem.at[12], yz(k)[1]).start()
    for k in range(1, opts):
        same(rx_v.at[opt], send_sem.at[13], recv_sem.at[13], xp(k)[1]).start()
        same(mc_v.at[opt], send_sem.at[14], recv_sem.at[14], xp(k)[1]).start()

    logp_v[...] = jnp.zeros_like(logp_v)
    logp_v[0:heads, :] = logs_ref[...]
    row_i = lax.broadcasted_iota(jnp.int32, (BLOCK, BLOCK), 0)
    col_i = lax.broadcasted_iota(jnp.int32, (BLOCK, BLOCK), 1)
    upper = jnp.where(row_i <= col_i, 1.0, 0.0).astype(F32)
    lower = jnp.where(row_i >= col_i, 1.0, 0.0).astype(F32)
    for b in range(2):
        part = logp_v[:, b * BLOCK : (b + 1) * BLOCK]
        r_v[b] = dot_nn(part, upper, HIGH)
        rt_v[b * BLOCK : (b + 1) * BLOCK, :] = dot_nt(lower, part, HIGH)

    mix_v[...] = jnp.zeros_like(mix_v)
    lane_i = lax.broadcasted_iota(jnp.int32, (2 * BLOCK, N), 1)

    def column(h):
        return jnp.sum(jnp.where(lane_i == h, rt_v[...], 0.0), axis=1, keepdims=True)

    half = BLOCK // 2
    tri_a = lax.broadcasted_iota(jnp.int32, (half, BLOCK), 1) >= lax.broadcasted_iota(jnp.int32, (half, BLOCK), 0)
    tri_b = lax.broadcasted_iota(jnp.int32, (half, half), 1) >= lax.broadcasted_iota(jnp.int32, (half, half), 0)

    def decays(rt, rs):
        top = jnp.exp(jnp.where(tri_a, rs - rt[0:half], -jnp.inf))
        bottom = jnp.exp(jnp.where(tri_b, rs[:, half:] - rt[half:], -jnp.inf))
        return top, bottom

    def mix_pair(hp, carry):
        adds = [[None, None], [None, None]]
        for j in range(2):
            h = hp * 2 + j
            lanes = pl.ds(pl.multiple_of(h * N, N), N)
            col = column(h)
            for b in range(2):
                at = pl.ds(b * BLOCK, BLOCK)
                xb = x_v[at, lanes]
                db = dy_v[at, lanes]
                rt = col[b * BLOCK : (b + 1) * BLOCK]
                rs = r_v[b, pl.ds(h, 1), :]
                prod = dot_nt(xb, db)
                top, bottom = decays(rt, rs)
                top = top * prod[0:half]
                bottom = bottom * prod[half:, half:]
                adds[b][0] = top if j == 0 else adds[b][0] + top
                adds[b][1] = bottom if j == 0 else adds[b][1] + bottom
                closing = rt[BLOCK - 1 : BLOCK]
                erow_v[b, :, lanes] = jnp.broadcast_to(jnp.exp(closing), (8, N))
                xs_v[at, lanes] = (xb.astype(F32) * jnp.exp(closing - rt)).astype(BF16)
                ds_v[at, lanes] = (db.astype(F32) * jnp.exp(rt)).astype(BF16)
        for b in range(2):
            mix_v[b, 0:half, :] += adds[b][0]
            mix_v[b, half:, half:] += adds[b][1]
        return carry

    pairs = heads // 2

    def mix_group(first_pair, last_pair):
        for g in range(groups):
            if first_pair <= g * (pairs // groups) < last_pair:
                for copy in in_copies(g):
                    copy.wait()
        lax.fori_loop(first_pair, last_pair, mix_pair, 0)

    cuts = (0, pairs // 8, pairs // 4, pairs * 3 // 8, pairs)
    mix_group(cuts[0], cuts[1])
    wait_bytes(w_v.at[0, 0, pl.ds(0, opts - 1), :, left], recv_sem.at[0])
    for k in far_first:
        same(w_v.at[chip, core, :, :, left], send_sem.at[2], blk_sem.at[k], yz(k)[1]).start()
    same(w_v.at[chip, core, :, :, left], send_sem.at[3], recv_sem.at[3], partner).start()
    wait_bytes(rx_v.at[pl.ds(0, opts - 1)], recv_sem.at[13])
    old_sum = rx_v[0]
    for k in range(1, opts):
        old_sum = old_sum + rx_v[k]
    dlo_v[...] = old_sum
    dlo_v[0:1, :] = rt_v[BLOCK - 1 : BLOCK, :] + rt_v[2 * BLOCK - 1 : 2 * BLOCK, :]
    remote(dlo_v, dlp_v, send_sem.at[1], recv_sem.at[1], partner).start()
    mix_group(cuts[1], cuts[2])
    wait_bytes(w_v.at[pl.ds(0, chips - 1), 0, 0, :, right], recv_sem.at[12])
    for k in range(1, opts):
        same(w_v.at[:, core, opt, :, right], send_sem.at[15], half_sem.at[k], xp(k)[1]).start()
    same(w_v.at[:, core, opt, :, right], send_sem.at[3], recv_sem.at[3], partner).start()
    mix_group(cuts[2], cuts[3])
    wait_bytes(dlp_v, recv_sem.at[1])
    dc_v[chip] = dlo_v[...] + dlp_v[...]
    for k in far_first:
        same(dc_v.at[chip], send_sem.at[4], recv_sem.at[4], yz(k)[1]).start()
    mix_group(cuts[3], cuts[4])
    for k in range(1, chips):
        block = w_v.at[owner_before(k), core, :, :, left]
        wait_bytes(block, blk_sem.at[k])
        same(block, send_sem.at[3], recv_sem.at[3], partner).start()
    for k in range(1, opts):
        block = w_v.at[:, core, (opt + opts - k) % opts, :, right]
        wait_bytes(block, half_sem.at[k])
        same(block, send_sem.at[3], recv_sem.at[3], partner).start()
    lay_copy.wait()
    wait_bytes(w_v.at[:, 0], recv_sem.at[3])

    proj = dot_nn(lay_v[...], w_v[...].reshape(dim, 2 * N)).astype(BF16)
    bc_v[...] = proj
    bct_v[...] = jnp.transpose(proj.astype(F32)).astype(BF16)
    for b in range(2):
        at = slice(b * BLOCK, (b + 1) * BLOCK)
        aff_v[b] = dot_nt(bc_v[at, 0:N], bc_v[at, N : 2 * N])

    def add_pair(k, carry):
        lanes = pl.ds(pl.multiple_of(owner_after(k) * 2 * N, 2 * N), 2 * N)
        e0 = erow_v[0, 0:1, lanes]
        e1 = erow_v[1, 0:1, lanes]
        f0 = dot_nn(bct_v[0:N, 0:BLOCK], xs_v[0:BLOCK, lanes])
        f1 = dot_nn(bct_v[0:N, BLOCK:], xs_v[BLOCK:, lanes])
        k0 = dot_nn(bct_v[N:, 0:BLOCK], ds_v[0:BLOCK, lanes])
        k1 = dot_nn(bct_v[N:, BLOCK:], ds_v[BLOCK:, lanes])
        f0_v[:, lanes] = f0
        k1_v[:, lanes] = k1
        state = (e1 * f0 + f1).astype(BF16)
        grad = (k0 + e0 * k1).astype(BF16)
        for j in range(2):
            t_v[j, k, 0] = state[:, j * N : (j + 1) * N]
            t_v[j, k, 1] = grad[:, j * N : (j + 1) * N]
        return carry

    lane_r = lax.broadcasted_iota(jnp.int32, (1, N), 1)

    def decay_of(ref, h):
        return jnp.exp(jnp.sum(jnp.where(lane_r == h, ref[0:1, :], 0.0), axis=1, keepdims=True))

    first = core == 0

    def combine(k, carry):
        h = 2 * owner_after(k) + core
        mine = decay_of(dlo_v, h)
        theirs = decay_of(dlp_v, h)
        one = jnp.ones_like(mine)
        own_f = t_v[core, k, 0].astype(F32)
        own_b = t_v[core, k, 1].astype(F32)
        oth_f = pt_v[k, 0].astype(F32)
        oth_b = pt_v[k, 1].astype(F32)
        state = jnp.where(first, theirs, one) * own_f + jnp.where(first, one, mine) * oth_f
        grad = jnp.where(first, one, theirs) * own_b + jnp.where(first, mine, one) * oth_b
        cb_v[k, 0] = state.astype(BF16)
        cb_v[k, 1] = grad.astype(BF16)
        return carry

    def piece(g):
        return chips - (g + 1) * fine

    def combine_group(g):
        at = pl.ds(piece(g), fine)
        wait_bytes(pt_v.at[at], d2d_sem.at[g])
        lax.fori_loop(piece(g), piece(g) + fine, combine, 0, unroll=True)
        for k in reversed(range(max(1, piece(g)), piece(g) + fine)):
            remote(cb_v.at[k], rb_v.at[chip], send_sem.at[6], recv_sem.at[6], yz(k)[1]).start()

    lag = 2
    for g in range(fines):
        lax.fori_loop(piece(g), piece(g) + fine, add_pair, 0, unroll=True)
        at = pl.ds(piece(g), fine)
        remote(t_v.at[1 - core, at], pt_v.at[at], send_sem.at[5], d2d_sem.at[g], partner).start()
        if g >= lag:
            combine_group(g - lag)
    for g in range(max(0, fines - lag), fines):
        combine_group(g)
    rb_v[chip] = cb_v[0]

    def inner_pair(hp, carry):
        for j in range(2):
            h = hp * 2 + j
            lanes = pl.ds(pl.multiple_of(h * N, N), N)
            col = column(h)
            gain = skip_ref[h]
            for b in range(2):
                rt = col[b * BLOCK : (b + 1) * BLOCK]
                rs = r_v[b, pl.ds(h, 1), :]
                top, bottom = decays(rt, rs)
                top = (top * aff_v[b, 0:half, :]).astype(BF16)
                bottom = (bottom * aff_v[b, half:, half:]).astype(BF16)
                db = dy_v[pl.ds(b * BLOCK, BLOCK), lanes]
                low = db[half:]
                gi_v[pl.ds(b * BLOCK, half), lanes] = (dot_nn(top, db) + gain * db[0:half].astype(F32)).astype(BF16)
                gi_v[pl.ds(b * BLOCK + half, half), lanes] = (dot_nn(bottom, low) + gain * low.astype(F32)).astype(BF16)
        return carry

    lax.fori_loop(0, heads // 2, inner_pair, 0)

    wait_bytes(dc_v.at[pl.ds(0, chips - 1)], recv_sem.at[4])
    wait_bytes(rb_v.at[pl.ds(0, chips - 1)], recv_sem.at[6])
    lane_c = lax.broadcasted_iota(jnp.int32, (chips, N), 1)
    chip_decay = jnp.exp(jnp.sum(jnp.where(lane_c == seq, dc_v[:, 0, :], 0.0), axis=1, keepdims=True))
    run = jnp.zeros((N, N), F32)
    for o in range(chips):
        ob_v[o, 0] = run.astype(BF16)
        run = chip_decay[o : o + 1] * run + rb_v[o, 0].astype(F32)
    run = jnp.zeros((N, N), F32)
    for o in reversed(range(chips)):
        ob_v[o, 1] = run.astype(BF16)
        run = chip_decay[o : o + 1] * run + rb_v[o, 1].astype(F32)
    for k in range(1, chips):
        other, dev = yz(k)
        remote(ob_v.at[other], ib_v.at[k], send_sem.at[7], entry_sem.at[k], dev).start()
    ib_v[0] = ob_v[chip]

    for b in range(2):
        at = slice(b * BLOCK, (b + 1) * BLOCK)
        mix = mix_v[b].astype(BF16)
        gbt_v[0:N, at] = dot_nt(bct_v[N:, at], mix)
        gbt_v[N:, at] = dot_nn(bct_v[0:N, at], mix)

    def entry(k, carry):
        h = 2 * owner_before(k) + core
        back = opposite(k)
        mine = decay_of(dlo_v, h)
        theirs = decay_of(dlp_v, h)
        one = jnp.ones_like(mine)
        nil = jnp.zeros_like(mine)
        state = ib_v[k, 0].astype(F32)
        grad = ib_v[k, 1].astype(F32)
        own_f = t_v[core, back, 0].astype(F32)
        own_b = t_v[core, back, 1].astype(F32)
        oth_f = pt_v[back, 0].astype(F32)
        oth_b = pt_v[back, 1].astype(F32)
        fin_v[core, k, 0] = (jnp.where(first, one, theirs) * state + jnp.where(first, nil, one) * oth_f).astype(BF16)
        fin_v[core, k, 1] = (jnp.where(first, theirs, one) * grad + jnp.where(first, one, nil) * oth_b).astype(BF16)
        xb_v[k, 0] = (jnp.where(first, mine, one) * state + jnp.where(first, one, nil) * own_f).astype(BF16)
        xb_v[k, 1] = (jnp.where(first, one, mine) * grad + jnp.where(first, nil, one) * own_b).astype(BF16)
        return carry

    def finish_pair(k, carry):
        o = owner_before(k)
        lanes = pl.ds(pl.multiple_of(o * 2 * N, 2 * N), 2 * N)
        e0 = erow_v[0, 0:1, lanes]
        e1 = erow_v[1, 0:1, lanes]
        s0 = jnp.concatenate([fin_v[0, k, 0], fin_v[1, k, 0]], axis=1)
        g1 = jnp.concatenate([fin_v[0, k, 1], fin_v[1, k, 1]], axis=1)
        s1 = (f0_v[:, lanes] + e0 * s0.astype(F32)).astype(BF16)
        g0 = (k1_v[:, lanes] + e1 * g1.astype(F32)).astype(BF16)
        cols = [column(2 * o), column(2 * o + 1)]
        for b, (st, gr) in enumerate(((s0, g0), (s1, g1))):
            at = slice(b * BLOCK, (b + 1) * BLOCK)
            gbt_v[0:N, at] += dot_nt(gr, xs_v[at, lanes])
            gbt_v[N:, at] += dot_nt(st, ds_v[at, lanes])
            outer = dot_nn(bc_v[at, 0:N], gr)
            for j in range(2):
                sub = pl.ds(pl.multiple_of((o * 2 + j) * N, N), N)
                rt = cols[j][at]
                shrink = jnp.exp(rt[BLOCK - 1 : BLOCK] - rt)
                gi_v[at, sub] = (gi_v[at, sub].astype(F32) + shrink * outer[:, j * N : (j + 1) * N]).astype(BF16)
        return carry

    def out_copy(k):
        lanes = pl.ds(pl.multiple_of(owner_before(k) * 2 * N, 2 * N), 2 * N)
        return pltpu.make_async_copy(gi_v.at[:, lanes], gi_hbm.at[:, lanes], out_sem.at[k])

    def finish_group(g):
        wait_bytes(xb_v.at[pl.ds(g * fine, fine)], fin_sem.at[g])
        lax.fori_loop(g * fine, (g + 1) * fine, finish_pair, 0, unroll=True)
        for k in range(g * fine, (g + 1) * fine):
            out_copy(k).start()

    for g in range(fines):
        at = pl.ds(g * fine, fine)
        for k in range(max(1, g * fine), (g + 1) * fine):
            wait_bytes(ib_v.at[k], entry_sem.at[k])
        lax.fori_loop(g * fine, (g + 1) * fine, entry, 0, unroll=True)
        remote(xb_v.at[at], fin_v.at[core, at], send_sem.at[8], fin_sem.at[g], partner).start()
        if g >= 1:
            finish_group(g - 1)
    finish_group(fines - 1)

    gbt_b = gbt_v[...].astype(BF16)

    def weight_pair(k, carry):
        lanes = pl.ds(pl.multiple_of(owner_after(k) * 2 * rblk, 2 * rblk), 2 * rblk)
        part = dot_nn(gbt_b, lay_v[:, lanes]).astype(BF16)
        wg_v[0, k] = part[:, 0:rblk]
        wg_v[1, k] = part[:, rblk:]
        return carry

    def chip_sum(k, carry):
        rss_v[k] = (wg_v[core, k].astype(F32) + rd_v[k].astype(F32)).astype(BF16)
        return carry

    def sum_group(g):
        at = pl.ds(piece(g), fine)
        wait_bytes(rd_v.at[at], rs_sem.at[g])
        lax.fori_loop(piece(g), piece(g) + fine, chip_sum, 0, unroll=True)
        for k in reversed(range(max(1, piece(g)), piece(g) + fine)):
            remote(rss_v.at[k], rsr_v.at[k], send_sem.at[10], recv_sem.at[10], yz(k)[1]).start()

    for g in range(fines):
        lax.fori_loop(piece(g), piece(g) + fine, weight_pair, 0, unroll=True)
        at = pl.ds(piece(g), fine)
        remote(wg_v.at[1 - core, at], rd_v.at[at], send_sem.at[9], rs_sem.at[g], partner).start()
        if g >= lag:
            sum_group(g - lag)
    for g in range(max(0, fines - lag), fines):
        sum_group(g)
    rsr_v[0] = rss_v[0]
    wait_bytes(rsr_v.at[pl.ds(0, chips - 1)], recv_sem.at[10])
    acc = rsr_v[0].astype(F32)
    for k in range(1, chips):
        acc = acc + rsr_v[k].astype(F32)
    xg_v[opt] = jnp.transpose(acc).astype(BF16)
    for k in range(1, opts):
        same(xg_v.at[opt], send_sem.at[11], recv_sem.at[11], xp(k)[1]).start()
    wait_bytes(mc_v.at[pl.ds(0, opts - 1)], recv_sem.at[14])
    wait_bytes(xg_v.at[pl.ds(0, opts - 1)], recv_sem.at[11])
    grad = xg_v[0].astype(F32)
    for k in range(1, opts):
        grad = grad + xg_v[k].astype(F32)
    gt_v[...] = grad

    def over_all(buf, row, base, combine_fn):
        buf[seq, 0:1] = row
        for k in range(1, seqs):
            same(buf.at[seq, 0:1], send_sem.at[base], recv_sem.at[base], ((seq + k) % seqs, opt)).start()
        wait_bytes(buf.at[pl.ds(0, seqs - 1), 0:1], recv_sem.at[base])
        value = buf[0, 0:1]
        for k in range(1, seqs):
            value = combine_fn(value, buf[k, 0:1])
        return value

    col_raw = over_all(s_v, jnp.sum(grad * grad, axis=0, keepdims=True), 16, jnp.add)
    raw_total = jnp.sum(col_raw, axis=1, keepdims=True)
    factor = jnp.minimum(1.0, clip_norm / jnp.sqrt(raw_total + norm_floor))

    def moment_of(code, part):
        return beta_one * code.astype(F32) * mscale_ref[...] + (1.0 - beta_one) * (part * factor)

    top = jnp.zeros((1, 2 * N), F32)
    for k in range(opts):
        part = moment_of(mc_v[k], gt_v[k * rows : (k + 1) * rows])
        top = jnp.maximum(top, jnp.max(jnp.abs(part), axis=0, keepdims=True))
    peak = over_all(m_v, top, 17, jnp.maximum)

    own = gt_v[pl.ds(pl.multiple_of(opt * rows, rows), rows), :]
    scaled = own * factor
    moment = moment_of(code_ref[...], own)
    squares = scaled * scaled
    old_total = jnp.sum(dc_v[:, 1, 0:1], axis=0, keepdims=True)
    col_next = beta_two * colstat_ref[...] + (1.0 - beta_two) * (factor * factor * col_raw / dim + tiny_square)
    eye = lax.broadcasted_iota(jnp.int32, (rows, rows), 0) == lax.broadcasted_iota(jnp.int32, (rows, rows), 1)
    old_col = jnp.sum(jnp.where(eye, jnp.broadcast_to(old_row, (rows, rows)), 0.0), axis=1, keepdims=True)
    row_next = beta_two * old_col + (1.0 - beta_two) * (
        jnp.sum(squares, axis=1, keepdims=True) / (2 * N) + tiny_square
    )
    row_mean = (
        beta_two * old_total + (1.0 - beta_two) * (factor * factor * raw_total / (2 * N) + dim * tiny_square)
    ) / dim
    second = row_next * col_next / row_mean
    upd_ref[...] = moment / (jnp.sqrt(second) + adam_floor) + weight_decay * w_ref[...]
    scale_next = peak + peak_floor
    scaleo_ref[...] = scale_next
    codeo_ref[...] = (moment / scale_next).astype(BF16)
    colo_ref[...] = col_next
    rowo_ref[...] = jnp.sum(jnp.where(eye, jnp.broadcast_to(row_next, (rows, rows)), 0.0), axis=0, keepdims=True)

    for k in range(chips):
        out_copy(k).wait()
    wait_bytes(w_v.at[0, 0, pl.ds(0, opts - 1), :, left], send_sem.at[0])
    wait_bytes(dlo_v, send_sem.at[1])
    wait_bytes(w_v.at[pl.ds(0, chips - 1), 0, :, :, left], send_sem.at[2])
    wait_bytes(w_v.at[:, 0], send_sem.at[3])
    wait_bytes(dc_v.at[pl.ds(0, chips - 1)], send_sem.at[4])
    wait_bytes(pt_v, send_sem.at[5])
    wait_bytes(cb_v.at[pl.ds(0, chips - 1)], send_sem.at[6])
    wait_bytes(ob_v.at[pl.ds(0, chips - 1)], send_sem.at[7])
    wait_bytes(xb_v, send_sem.at[8])
    wait_bytes(rd_v, send_sem.at[9])
    wait_bytes(rss_v.at[pl.ds(0, chips - 1)], send_sem.at[10])
    wait_bytes(xg_v.at[pl.ds(0, opts - 1)], send_sem.at[11])
    wait_bytes(w_v.at[pl.ds(0, chips - 1), 0, 0, :, right], send_sem.at[12])
    wait_bytes(rx_v.at[pl.ds(0, opts - 1)], send_sem.at[13])
    wait_bytes(mc_v.at[pl.ds(0, opts - 1)], send_sem.at[14])
    wait_bytes(w_v.at[:, 0, pl.ds(0, opts - 1), :, right], send_sem.at[15])
    for base, buf in ((16, s_v), (17, m_v)):
        wait_bytes(buf.at[pl.ds(0, seqs - 1), 0:1], send_sem.at[base])


def copy_out(gi_hbm, upd_ref, code_ref, scale_ref, row_ref, col_ref, gi_out, upd_o, code_o, scale_o, row_o, col_o, held, i_sem, o_sem):
    pieces = i_sem.shape[0]
    size = held.shape[0] // pieces

    def move(source, target, k, sem):
        at = pl.ds(k * size, size)
        return pltpu.make_async_copy(source.at[at], target.at[at], sem.at[k])

    for k in range(pieces):
        move(gi_hbm, held, k, i_sem).start()
    upd_o[...] = upd_ref[...]
    code_o[...] = code_ref[...]
    scale_o[...] = scale_ref[...]
    row_o[...] = row_ref[...]
    col_o[...] = col_ref[...]
    for k in range(pieces):
        move(gi_hbm, held, k, i_sem).wait()
        move(held, gi_out, k, o_sem).start()
    for k in range(pieces):
        move(held, gi_out, k, o_sem).wait()


def per_device(
    seqs, opts, layer_in, ssm_input, grad_out, log_decay, skip_gain, w_bc, m_code, m_scale, row_stat, col_stat
):
    heads = skip_gain.shape[0]
    tokens, width = ssm_input.shape[1:]
    dim = layer_in.shape[2]
    rows = w_bc.shape[0]
    chips = seqs // 2
    rblk = rows * opts
    vm = pl.BlockSpec(memory_space=pltpu.VMEM)
    hbm = pl.BlockSpec(memory_space=pl.ANY)
    state = (chips, 2, N, N)
    scratch = [
        pltpu.VMEM((tokens, width), BF16),
        pltpu.VMEM((tokens, width), BF16),
        pltpu.VMEM((tokens, dim), BF16),
        pltpu.VMEM((tokens, width), BF16),
        pltpu.VMEM((tokens, width), BF16),
        pltpu.VMEM((tokens, width), BF16),
        pltpu.VMEM((chips, 2, opts, rows, 2 * N), BF16),
        pltpu.VMEM((N, tokens), F32),
        pltpu.VMEM((2, N, BLOCK), F32),
        pltpu.VMEM((tokens, N), F32),
        pltpu.VMEM((2, 8, width), F32),
        pltpu.VMEM((2, BLOCK, BLOCK), F32),
        pltpu.VMEM((2, BLOCK, BLOCK), F32),
        pltpu.VMEM((tokens, 2 * N), BF16),
        pltpu.VMEM((2 * N, tokens), BF16),
        pltpu.VMEM((N, width), F32),
        pltpu.VMEM((N, width), F32),
        pltpu.VMEM((2,) + state, BF16),
        pltpu.VMEM(state, BF16),
        pltpu.VMEM(state, BF16),
        pltpu.VMEM(state, BF16),
        pltpu.VMEM(state, BF16),
        pltpu.VMEM(state, BF16),
        pltpu.VMEM(state, BF16),
        pltpu.VMEM((2,) + state, BF16),
        pltpu.VMEM((2 * N, tokens), F32),
        pltpu.VMEM((2, chips, 2 * N, rblk), BF16),
        pltpu.VMEM((chips, 2 * N, rblk), BF16),
        pltpu.VMEM((chips, 2 * N, rblk), BF16),
        pltpu.VMEM((chips, 2 * N, rblk), BF16),
        pltpu.VMEM((opts, rblk, 2 * N), BF16),
        pltpu.VMEM((rblk, 2 * N), F32),
        pltpu.VMEM((opts, rows, 2 * N), BF16),
        pltpu.VMEM((opts, 8, N), F32),
        pltpu.VMEM((8, N), F32),
        pltpu.VMEM((8, N), F32),
        pltpu.VMEM((chips, 8, N), F32),
        pltpu.VMEM((seqs, 8, 2 * N), F32),
        pltpu.VMEM((seqs, 8, 2 * N), F32),
        pltpu.SemaphoreType.DMA((9,)),
        pltpu.SemaphoreType.DMA((chips,)),
        pltpu.SemaphoreType.DMA((18,)),
        pltpu.SemaphoreType.DMA((18,)),
        pltpu.SemaphoreType.DMA((chips,)),
        pltpu.SemaphoreType.DMA((opts,)),
        pltpu.SemaphoreType.DMA((chips,)),
        pltpu.SemaphoreType.DMA((min(8, chips),)),
        pltpu.SemaphoreType.DMA((min(8, chips),)),
        pltpu.SemaphoreType.DMA((min(8, chips),)),
    ]
    shapes = (
        jax.ShapeDtypeStruct((tokens, width), BF16),
        jax.ShapeDtypeStruct((rows, 2 * N), F32),
        jax.ShapeDtypeStruct((rows, 2 * N), BF16),
        jax.ShapeDtypeStruct((1, 2 * N), F32),
        jax.ShapeDtypeStruct((1, rows), F32),
        jax.ShapeDtypeStruct((1, 2 * N), F32),
    )
    out = pl.pallas_call(
        functools.partial(kernel, seqs, opts),
        out_shape=shapes,
        in_specs=[hbm, hbm, hbm, vm, pl.BlockSpec(memory_space=pltpu.SMEM), vm, vm, vm, vm, vm],
        out_specs=(hbm, vm, vm, vm, vm, vm),
        scratch_shapes=scratch,
        compiler_params=pltpu.CompilerParams(
            collective_id=0, has_side_effects=True, vmem_limit_bytes=66_000_000
        ),
    )(
        ssm_input[0],
        grad_out[0],
        layer_in[0],
        log_decay[0],
        skip_gain,
        w_bc,
        m_code,
        m_scale.reshape(1, 2 * N),
        row_stat.reshape(1, rows),
        col_stat.reshape(1, 2 * N),
    )
    out = pl.pallas_call(
        copy_out,
        out_shape=shapes,
        in_specs=[hbm, vm, vm, vm, vm, vm],
        out_specs=(hbm, vm, vm, vm, vm, vm),
        scratch_shapes=[
            pltpu.VMEM((tokens, width), BF16),
            pltpu.SemaphoreType.DMA((8,)),
            pltpu.SemaphoreType.DMA((8,)),
        ],
    )(*out)
    grad_input, update, code_next, scale_next, row_next, col_next = out
    return (
        grad_input[None],
        update,
        code_next,
        scale_next.reshape(2 * N),
        row_next.reshape(rows),
        col_next.reshape(2 * N),
    )


def solution(mesh):
    both = ("seq", "opt")
    return jax.shard_map(
        functools.partial(per_device, mesh.shape["seq"], mesh.shape["opt"]),
        mesh=mesh,
        in_specs=(
            P("opt", "seq", None),
            P("opt", "seq", None),
            P("opt", "seq", None),
            P("opt", None, "seq"),
            P(),
            P(both, None),
            P(both, None),
            P(),
            P(both),
            P(),
        ),
        out_specs=(P("opt", "seq", None), P(both, None), P(both, None), P(), P(both), P()),
        check_vma=False,
    )
```

time: 128 us -> 102 us (0.80)
  Pallas kernels: 119 us -> 101 us
  local copies, waits for them, and re-layouts: 7.58 us -> 0 us
    pallas_call x1 -> x2, Pallas kernels: 119 us -> 101 us  [the longest x1 95.7 us: per_device(): pl.pallas_call(functools.partial(kernel, seqs, opts), out_shape=shapes, i...]
    unnamed x16 -> x0, local copies, waits for them, and re-layouts: 7.58 us -> none
where the time goes in v2:
time: 102 us; the launch traced here: 101 us
  Pallas kernels  101 us (99%)
    pallas_call x1, Pallas kernels, per_device(): pl.pallas_call(functools.partial(kernel, seqs, opts), out_shape=shapes, i...  95.7 us
    pallas_call x1, Pallas kernels, per_device(): pl.pallas_call(copy_out, out_shape=shapes, in_specs=[hbm, vm, vm, vm, vm,...  4.99 us

profile of v2, /device:TPU:1, one launch (start us, length us, event | category | flops | bytes accessed | tf_op | source)
XLA Modules:
  0.0 101.5 jit_solution(17567562828110029245)
XLA Ops:
  0.6 95.7 %shard_map.145 = (bf16[512,4096]{1,0:T(8,128)(2,1)}, f32[32,256]{1,0:T(8,128)}, bf16[32,256]{1,0:T(8,128)(2,1)}, f32[1,256]{1,0:T(1,128)}, f32[1,32]{1,0:T(1,128)}, /*index=5*/f32[1,256]{1,0:T(1,128)}) custom-call(bf16[512,4096]{1,0:T(8,128)(2,1)} %bitcast.11, bf16[512,4096]{1,0:T(8,128)(2,1)} %bitcast.12, bf16[512,4096]{1,0:T(8,128)(2,1)} %bitcast.13, ...), custom_call_target="tpu_custom_call" | custom-call | tf_op jit(solution)/shard_map/pallas_call | solution.py:673
  96.3 5.0 %shard_map.146 = (bf16[512,4096]{1,0:T(8,128)(2,1)}, f32[32,256]{1,0:T(8,128)}, bf16[32,256]{1,0:T(8,128)(2,1)}, f32[1,256]{1,0:T(1,128)}, f32[1,32]{1,0:T(1,128)}, /*index=5*/f32[1,256]{1,0:T(1,128)}) custom-call(bf16[512,4096]{1,0:T(8,128)(2,1)} %get-tuple-element.18.gi_hbm, f32[32,256]{1,0:T(8,128)} %get-tuple-element.19.upd_ref, ...), custom_call_target="tpu_custom_call" | custom-call | tf_op jit(solution)/shard_map/pallas_call | solution.py:694

commit v3 on v2

v3 whole, which is shorter than its diff:
```python
import functools
import math

import jax
import jax.numpy as jnp
from jax import lax
from jax.experimental import pallas as pl
from jax.experimental.pallas import tpu as pltpu
from jax.sharding import PartitionSpec as P

MESH = pl.DeviceIdType.MESH
BLOCK = 256
N = 128
F32 = jnp.float32
BF16 = jnp.bfloat16
HIGH = lax.Precision.HIGHEST

beta_one = 0.9
beta_two = 0.95
weight_decay = 0.1
clip_norm = 1.0
tiny_square = 1e-30
adam_floor = 1e-08
peak_floor = 1e-06
norm_floor = 1e-06


def dot_nn(a, b, precision=None):
    return lax.dot_general(a, b, (((1,), (0,)), ((), ())), preferred_element_type=F32, precision=precision)


def dot_nt(a, b, precision=None):
    return lax.dot_general(a, b, (((1,), (1,)), ((), ())), preferred_element_type=F32, precision=precision)


def kernel(
    seqs,
    opts,
    x_hbm,
    dy_hbm,
    lay_hbm,
    logs_hbm,
    skip_hbm,
    w_hbm,
    code_hbm,
    mscale_hbm,
    rowstat_hbm,
    colstat_hbm,
    gi_v,
    upd_ref,
    codeo_ref,
    scaleo_ref,
    rowo_ref,
    colo_ref,
    x_v,
    dy_v,
    lay_v,
    xs_v,
    ds_v,
    wl_v,
    wr_v,
    logp_v,
    skip_ref,
    w_ref,
    mscale_ref,
    rowstat_ref,
    colstat_ref,
    r_v,
    rt_v,
    erow_v,
    mix_v,
    aff_v,
    bc_v,
    bct_v,
    f0_v,
    k1_v,
    t_v,
    pt_v,
    cb_v,
    rb_v,
    ob_v,
    ib_v,
    xb_v,
    fin_v,
    gbt_v,
    wg_v,
    rd_v,
    rss_v,
    rsr_v,
    bx_v,
    by_v,
    bz_v,
    bw_v,
    xg_v,
    gt_v,
    mc_v,
    rx_v,
    dlo_v,
    dlp_v,
    dc_v,
    s_v,
    m_v,
    in_sem,
    small_sem,
    send_sem,
    recv_sem,
    blk_sem,
    half_sem,
    entry_sem,
    d2d_sem,
    fin_sem,
    rs_sem,
):
    heads = skip_ref.shape[1]
    chips = seqs // 2
    rows = w_ref.shape[0]
    rblk = rows * opts
    width = x_hbm.shape[1]
    dim = lay_hbm.shape[1]
    groups = 4
    lanes_g = width // groups
    fines = min(8, chips)
    fine = chips // fines
    parts = 4
    per = chips // parts

    seq = lax.axis_index("seq")
    opt = lax.axis_index("opt")
    chip = seq // 2
    core = seq % 2
    mate = chip * 2 + (1 - core)
    partner = (mate, opt)

    side = math.isqrt(chips)

    def step_of(i):
        return (i * (i + 1) // 2) % side

    def owner_after(e):
        zs = (chip // side + step_of(e // side)) % side
        ys = (chip % side + step_of(e % side)) % side
        return zs * side + ys

    def owner_before(e):
        zs = (chip // side + side - step_of(e // side)) % side
        ys = (chip % side + side - step_of(e % side)) % side
        return zs * side + ys

    def flip(i):
        return 2 * (i % 2) + i // 2 if side == 4 else i

    def opposite(e):
        return flip(e // side) * side + flip(e % side)

    far_first = tuple(range(chips - 1, 0, -1))

    def yz(e):
        other = owner_after(e)
        return other, (other * 2 + core, opt)

    def xp(k):
        other = (opt + k) % opts
        return other, (seq, other)

    def remote(src, dst, s_sem, r_sem, dev):
        return pltpu.make_async_remote_copy(
            src_ref=src, dst_ref=dst, send_sem=s_sem, recv_sem=r_sem, device_id=dev, device_id_type=MESH
        )

    def wait_bytes(ref, sem):
        pltpu.make_async_copy(ref, ref, sem).wait()

    def in_copies(g):
        lanes = pl.ds(g * lanes_g, lanes_g)
        return (
            pltpu.make_async_copy(x_hbm.at[:, lanes], x_v.at[:, lanes], in_sem.at[2 * g]),
            pltpu.make_async_copy(dy_hbm.at[:, lanes], dy_v.at[:, lanes], in_sem.at[2 * g + 1]),
        )

    lay_copy = pltpu.make_async_copy(lay_hbm, lay_v, in_sem.at[2 * groups])

    barrier = pltpu.get_barrier_semaphore()
    for k in range(1, seqs):
        pl.semaphore_signal(barrier, inc=1, device_id=((seq + k) % seqs, opt), device_id_type=MESH)
    for k in range(1, opts):
        pl.semaphore_signal(barrier, inc=1, device_id=xp(k)[1], device_id_type=MESH)

    def small(source, target, k):
        return pltpu.make_async_copy(source, target, small_sem.at[k])

    smalls = [
        small(w_hbm, w_ref, 0),
        small(rowstat_hbm, rowstat_ref, 1),
        small(code_hbm, mc_v.at[opt], 2),
        small(logs_hbm, logp_v.at[pl.ds(0, heads)], 3),
        small(skip_hbm, skip_ref, 4),
        small(mscale_hbm, mscale_ref, 5),
        small(colstat_hbm, colstat_ref, 6),
    ]
    for copy in smalls:
        copy.start()
    for g in range(groups):
        for copy in in_copies(g):
            copy.start()
    lay_copy.start()
    if heads < N:
        logp_v[heads:, :] = jnp.zeros((N - heads, logp_v.shape[1]), F32)

    for copy in smalls:
        copy.wait()
    wl_v[chip, core, opt] = w_ref[:, 0:N].astype(BF16)
    wr_v[chip, core, opt] = w_ref[:, N:].astype(BF16)
    old_row = rowstat_ref[...]
    rx_v[opt] = jnp.broadcast_to(jnp.sum(old_row, axis=1, keepdims=True), (8, N))


    def same(ref, s_sem, r_sem, dev):
        return remote(ref, ref, s_sem, r_sem, dev)

    pl.semaphore_wait(barrier, seqs - 1 + opts - 1)
    for k in range(1, opts):
        same(wl_v.at[chip, core, opt], send_sem.at[0], recv_sem.at[0], xp(k)[1]).start()
    for k in far_first:
        same(wr_v.at[chip, core, opt], send_sem.at[12], recv_sem.at[12], yz(k)[1]).start()
    for k in range(1, opts):
        same(rx_v.at[opt], send_sem.at[13], recv_sem.at[13], xp(k)[1]).start()
        same(mc_v.at[opt], send_sem.at[14], recv_sem.at[14], xp(k)[1]).start()

    row_i = lax.broadcasted_iota(jnp.int32, (BLOCK, BLOCK), 0)
    col_i = lax.broadcasted_iota(jnp.int32, (BLOCK, BLOCK), 1)
    upper = jnp.where(row_i <= col_i, 1.0, 0.0).astype(F32)
    lower = jnp.where(row_i >= col_i, 1.0, 0.0).astype(F32)
    for b in range(2):
        part = logp_v[:, b * BLOCK : (b + 1) * BLOCK]
        r_v[b] = dot_nn(part, upper, HIGH)
        rt_v[b * BLOCK : (b + 1) * BLOCK, :] = dot_nt(lower, part, HIGH)

    mix_v[...] = jnp.zeros_like(mix_v)
    lane_i = lax.broadcasted_iota(jnp.int32, (2 * BLOCK, N), 1)

    def column(h):
        return jnp.sum(jnp.where(lane_i == h, rt_v[...], 0.0), axis=1, keepdims=True)

    half = BLOCK // 2
    tri_a = lax.broadcasted_iota(jnp.int32, (half, BLOCK), 1) >= lax.broadcasted_iota(jnp.int32, (half, BLOCK), 0)
    tri_b = lax.broadcasted_iota(jnp.int32, (half, half), 1) >= lax.broadcasted_iota(jnp.int32, (half, half), 0)

    def decays(rt, rs):
        top = jnp.exp(jnp.where(tri_a, rs - rt[0:half], -jnp.inf))
        bottom = jnp.exp(jnp.where(tri_b, rs[:, half:] - rt[half:], -jnp.inf))
        return top, bottom

    def mix_pair(hp, carry):
        adds = [[None, None], [None, None]]
        for j in range(2):
            h = hp * 2 + j
            lanes = pl.ds(pl.multiple_of(h * N, N), N)
            col = column(h)
            for b in range(2):
                at = pl.ds(b * BLOCK, BLOCK)
                xb = x_v[at, lanes]
                db = dy_v[at, lanes]
                rt = col[b * BLOCK : (b + 1) * BLOCK]
                rs = r_v[b, pl.ds(h, 1), :]
                prod = dot_nt(xb, db)
                top, bottom = decays(rt, rs)
                top = top * prod[0:half]
                bottom = bottom * prod[half:, half:]
                adds[b][0] = top if j == 0 else adds[b][0] + top
                adds[b][1] = bottom if j == 0 else adds[b][1] + bottom
                closing = rt[BLOCK - 1 : BLOCK]
                erow_v[b, :, lanes] = jnp.broadcast_to(jnp.exp(closing), (8, N))
                xs_v[at, lanes] = (xb.astype(F32) * jnp.exp(closing - rt)).astype(BF16)
                ds_v[at, lanes] = (db.astype(F32) * jnp.exp(rt)).astype(BF16)
        for b in range(2):
            mix_v[b, 0:half, :] += adds[b][0]
            mix_v[b, half:, half:] += adds[b][1]
        return carry

    pairs = heads // 2

    def mix_group(first_pair, last_pair):
        for g in range(groups):
            if first_pair <= g * (pairs // groups) < last_pair:
                for copy in in_copies(g):
                    copy.wait()
        lax.fori_loop(first_pair, last_pair, mix_pair, 0)

    cuts = (0, pairs // 8, pairs // 4, pairs * 3 // 8, pairs)
    mix_group(cuts[0], cuts[1])
    wait_bytes(wl_v.at[0, 0, pl.ds(0, opts - 1)], recv_sem.at[0])
    for k in far_first:
        same(wl_v.at[chip, core, :], send_sem.at[2], blk_sem.at[k], yz(k)[1]).start()
    same(wl_v.at[chip, core, :], send_sem.at[3], recv_sem.at[3], partner).start()
    wait_bytes(rx_v.at[pl.ds(0, opts - 1)], recv_sem.at[13])
    old_sum = rx_v[0]
    for k in range(1, opts):
        old_sum = old_sum + rx_v[k]
    dlo_v[...] = old_sum
    dlo_v[0:1, :] = rt_v[BLOCK - 1 : BLOCK, :] + rt_v[2 * BLOCK - 1 : 2 * BLOCK, :]
    remote(dlo_v, dlp_v, send_sem.at[1], recv_sem.at[1], partner).start()
    mix_group(cuts[1], cuts[2])
    wait_bytes(wr_v.at[pl.ds(0, chips - 1), 0, 0], recv_sem.at[12])
    for k in range(1, opts):
        same(wr_v.at[:, core, opt], send_sem.at[15], half_sem.at[k], xp(k)[1]).start()
    same(wr_v.at[:, core, opt], send_sem.at[3], recv_sem.at[3], partner).start()
    mix_group(cuts[2], cuts[3])
    wait_bytes(dlp_v, recv_sem.at[1])
    dc_v[chip] = dlo_v[...] + dlp_v[...]
    for k in far_first:
        same(dc_v.at[chip], send_sem.at[4], recv_sem.at[4], yz(k)[1]).start()
    mix_group(cuts[3], cuts[4])
    for k in range(1, chips):
        block = wl_v.at[owner_before(k), core, :]
        wait_bytes(block, blk_sem.at[k])
        same(block, send_sem.at[3], recv_sem.at[3], partner).start()
    for k in range(1, opts):
        block = wr_v.at[:, core, (opt + opts - k) % opts]
        wait_bytes(block, half_sem.at[k])
        same(block, send_sem.at[3], recv_sem.at[3], partner).start()
    lay_copy.wait()
    wait_bytes(wl_v, recv_sem.at[3])

    proj = dot_nn(lay_v[...], jnp.concatenate([wl_v[...].reshape(dim, N), wr_v[...].reshape(dim, N)], axis=1)).astype(BF16)
    bc_v[...] = proj
    bct_v[...] = jnp.transpose(proj.astype(F32)).astype(BF16)
    for b in range(2):
        at = slice(b * BLOCK, (b + 1) * BLOCK)
        aff_v[b] = dot_nt(bc_v[at, 0:N], bc_v[at, N : 2 * N])

    def add_pair(way, k, carry):
        lanes = pl.ds(pl.multiple_of(owner_after(k) * 2 * N, 2 * N), 2 * N)
        if way == 0:
            first_blk = dot_nn(bct_v[0:N, 0:BLOCK], xs_v[0:BLOCK, lanes])
            second_blk = dot_nn(bct_v[0:N, BLOCK:], xs_v[BLOCK:, lanes])
            f0_v[:, lanes] = first_blk
            both = (erow_v[1, 0:1, lanes] * first_blk + second_blk).astype(BF16)
        else:
            first_blk = dot_nn(bct_v[N:, 0:BLOCK], ds_v[0:BLOCK, lanes])
            second_blk = dot_nn(bct_v[N:, BLOCK:], ds_v[BLOCK:, lanes])
            k1_v[:, lanes] = second_blk
            both = (first_blk + erow_v[0, 0:1, lanes] * second_blk).astype(BF16)
        for j in range(2):
            t_v[way, j, k] = both[:, j * N : (j + 1) * N]
        return carry

    lane_r = lax.broadcasted_iota(jnp.int32, (1, N), 1)

    def decay_of(ref, h):
        return jnp.exp(jnp.sum(jnp.where(lane_r == h, ref[0:1, :], 0.0), axis=1, keepdims=True))

    first = core == 0

    def combine(way, k, carry):
        h = 2 * owner_after(k) + core
        mine = decay_of(dlo_v, h)
        theirs = decay_of(dlp_v, h)
        one = jnp.ones_like(mine)
        own = t_v[way, core, k].astype(F32)
        other = pt_v[way, k].astype(F32)
        if way == 0:
            both = jnp.where(first, theirs, one) * own + jnp.where(first, one, mine) * other
        else:
            both = jnp.where(first, one, theirs) * own + jnp.where(first, mine, one) * other
        cb_v[way, k] = both.astype(BF16)
        return carry

    def piece(g, size):
        return chips - (g + 1) * size

    def combine_group(way, g):
        start = piece(g, per)
        at = pl.ds(start, per)
        wait_bytes(pt_v.at[way, at], d2d_sem.at[way, g])
        lax.fori_loop(start, start + per, functools.partial(combine, way), 0, unroll=True)
        for k in reversed(range(max(1, start), start + per)):
            remote(cb_v.at[way, k], rb_v.at[way, chip], send_sem.at[6], recv_sem.at[6 + way], yz(k)[1]).start()

    steps = [(way, g) for way in range(2) for g in range(parts)]
    for i, (way, g) in enumerate(steps):
        start = piece(g, per)
        at = pl.ds(start, per)
        lax.fori_loop(start, start + per, functools.partial(add_pair, way), 0, unroll=True)
        remote(t_v.at[way, 1 - core, at], pt_v.at[way, at], send_sem.at[5], d2d_sem.at[way, g], partner).start()
        if i >= 2:
            combine_group(*steps[i - 2])
    for i in range(len(steps) - 2, len(steps)):
        combine_group(*steps[i])
    for way in range(2):
        rb_v[way, chip] = cb_v[way, 0]

    lane_h = lax.broadcasted_iota(jnp.int32, (1, heads), 1)

    def inner_pair(hp, carry):
        for j in range(2):
            h = hp * 2 + j
            lanes = pl.ds(pl.multiple_of(h * N, N), N)
            col = column(h)
            gain = jnp.sum(jnp.where(lane_h == h, skip_ref[...], 0.0), axis=1, keepdims=True)
            for b in range(2):
                rt = col[b * BLOCK : (b + 1) * BLOCK]
                rs = r_v[b, pl.ds(h, 1), :]
                top, bottom = decays(rt, rs)
                top = (top * aff_v[b, 0:half, :]).astype(BF16)
                bottom = (bottom * aff_v[b, half:, half:]).astype(BF16)
                db = dy_v[pl.ds(b * BLOCK, BLOCK), lanes]
                low = db[half:]
                gi_v[pl.ds(b * BLOCK, half), lanes] = (dot_nn(top, db) + gain * db[0:half].astype(F32)).astype(BF16)
                gi_v[pl.ds(b * BLOCK + half, half), lanes] = (dot_nn(bottom, low) + gain * low.astype(F32)).astype(BF16)
        return carry

    lane_c = lax.broadcasted_iota(jnp.int32, (chips, N), 1)

    def scan_chips(way):
        wait_bytes(rb_v.at[way, pl.ds(0, chips - 1)], recv_sem.at[6 + way])
        chip_decay = jnp.exp(jnp.sum(jnp.where(lane_c == seq, dc_v[:, 0, :], 0.0), axis=1, keepdims=True))
        run = jnp.zeros((N, N), F32)
        for o in range(chips) if way == 0 else reversed(range(chips)):
            ob_v[way, o] = run.astype(BF16)
            run = chip_decay[o : o + 1] * run + rb_v[way, o].astype(F32)
        for k in far_first:
            other, dev = yz(k)
            remote(ob_v.at[way, other], ib_v.at[way, k], send_sem.at[7], entry_sem.at[way, k], dev).start()
        ib_v[way, 0] = ob_v[way, chip]

    lax.fori_loop(0, heads // 4, inner_pair, 0)
    wait_bytes(dc_v.at[pl.ds(0, chips - 1)], recv_sem.at[4])
    scan_chips(0)
    lax.fori_loop(heads // 4, heads // 2, inner_pair, 0)
    scan_chips(1)

    for b in range(2):
        at = slice(b * BLOCK, (b + 1) * BLOCK)
        mix = mix_v[b].astype(BF16)
        gbt_v[0:N, at] = dot_nt(bct_v[N:, at], mix)
        gbt_v[N:, at] = dot_nn(bct_v[0:N, at], mix)

    def entry(way, k, carry):
        h = 2 * owner_before(k) + core
        back = opposite(k)
        mine = decay_of(dlo_v, h)
        theirs = decay_of(dlp_v, h)
        one = jnp.ones_like(mine)
        nil = jnp.zeros_like(mine)
        came = ib_v[way, k].astype(F32)
        own = t_v[way, core, back].astype(F32)
        other = pt_v[way, back].astype(F32)
        if way == 0:
            here = jnp.where(first, one, theirs) * came + jnp.where(first, nil, one) * other
            there = jnp.where(first, mine, one) * came + jnp.where(first, one, nil) * own
        else:
            here = jnp.where(first, theirs, one) * came + jnp.where(first, one, nil) * other
            there = jnp.where(first, one, mine) * came + jnp.where(first, nil, one) * own
        fin_v[way, core, k] = here.astype(BF16)
        xb_v[way, k] = there.astype(BF16)
        return carry

    def finish_pair(way, k, carry):
        o = owner_before(k)
        lanes = pl.ds(pl.multiple_of(o * 2 * N, 2 * N), 2 * N)
        came = jnp.concatenate([fin_v[way, 0, k], fin_v[way, 1, k]], axis=1)
        if way == 0:
            later = (f0_v[:, lanes] + erow_v[0, 0:1, lanes] * came.astype(F32)).astype(BF16)
            for b, st in enumerate((came, later)):
                at = slice(b * BLOCK, (b + 1) * BLOCK)
                gbt_v[N:, at] += dot_nt(st, ds_v[at, lanes])
            return carry
        earlier = (k1_v[:, lanes] + erow_v[1, 0:1, lanes] * came.astype(F32)).astype(BF16)
        for b, gr in enumerate((earlier, came)):
            at = slice(b * BLOCK, (b + 1) * BLOCK)
            gbt_v[0:N, at] += dot_nt(gr, xs_v[at, lanes])
        return carry

    def outer_pair(k, carry):
        o = owner_before(k)
        lanes = pl.ds(pl.multiple_of(o * 2 * N, 2 * N), 2 * N)
        came = jnp.concatenate([fin_v[1, 0, k], fin_v[1, 1, k]], axis=1)
        earlier = (k1_v[:, lanes] + erow_v[1, 0:1, lanes] * came.astype(F32)).astype(BF16)
        cols = [column(2 * o), column(2 * o + 1)]
        for b, gr in enumerate((earlier, came)):
            at = slice(b * BLOCK, (b + 1) * BLOCK)
            outer = dot_nn(bc_v[at, 0:N], gr)
            for j in range(2):
                sub = pl.ds(pl.multiple_of((o * 2 + j) * N, N), N)
                rt = cols[j][at]
                shrink = jnp.exp(rt[BLOCK - 1 : BLOCK] - rt)
                gi_v[at, sub] = (gi_v[at, sub].astype(F32) + shrink * outer[:, j * N : (j + 1) * N]).astype(BF16)
        return carry

    def finish_group(way, g):
        start = piece(g, fine)
        wait_bytes(xb_v.at[way, pl.ds(start, fine)], fin_sem.at[way, g])
        lax.fori_loop(start, start + fine, functools.partial(finish_pair, way), 0, unroll=True)

    steps = [(way, g) for way in range(2) for g in range(fines)]
    behind = 3
    for i, (way, g) in enumerate(steps):
        start = piece(g, fine)
        at = pl.ds(start, fine)
        for k in reversed(range(max(1, start), start + fine)):
            wait_bytes(ib_v.at[way, k], entry_sem.at[way, k])
        lax.fori_loop(start, start + fine, functools.partial(entry, way), 0, unroll=True)
        remote(xb_v.at[way, at], fin_v.at[way, core, at], send_sem.at[8], fin_sem.at[way, g], partner).start()
        if i >= behind:
            finish_group(*steps[i - behind])
    for i in range(max(0, len(steps) - behind), len(steps)):
        finish_group(*steps[i])

    gbt_b = gbt_v[...].astype(BF16)

    def weight_pair(k, carry):
        lanes = pl.ds(pl.multiple_of(owner_after(k) * 2 * rblk, 2 * rblk), 2 * rblk)
        part = dot_nn(gbt_b, lay_v[:, lanes]).astype(BF16)
        wg_v[0, k] = part[:, 0:rblk]
        wg_v[1, k] = part[:, rblk:]
        return carry

    def chip_sum(k, carry):
        rss_v[k] = (wg_v[core, k].astype(F32) + rd_v[k].astype(F32)).astype(BF16)
        return carry

    cols = 2 * N
    main = cols * 3 // 4
    share = (cols - main) // opts

    def quarter(who):
        return pl.ds(pl.multiple_of(main + who * share, share), share)

    def sum_group(g):
        start = piece(g, fine)
        at = pl.ds(start, fine)
        wait_bytes(rd_v.at[at], rs_sem.at[g])
        lax.fori_loop(start, start + fine, chip_sum, 0, unroll=True)
        for k in reversed(range(max(1, start), start + fine)):
            top = pl.ds(0, main)
            remote(rss_v.at[k, top], rsr_v.at[k], send_sem.at[10], recv_sem.at[10], yz(k)[1]).start()
        if (g + 1) * 2 % fines == 0:
            half_at = pl.ds(start, chips // 2)
            for k in range(1, opts):
                other, dev = xp(k)
                remote(
                    rss_v.at[half_at, quarter(other)], bx_v.at[opt, half_at], send_sem.at[18], recv_sem.at[18], dev
                ).start()

    lag = 2
    for g in range(fines):
        start = piece(g, fine)
        at = pl.ds(start, fine)
        lax.fori_loop(start, start + fine, weight_pair, 0, unroll=True)
        remote(wg_v.at[1 - core, at], rd_v.at[at], send_sem.at[9], rs_sem.at[g], partner).start()
        if g >= lag:
            sum_group(g - lag)
    for g in range(max(0, fines - lag), fines):
        sum_group(g)
    rsr_v[0] = rss_v[0, 0:main]
    bx_v[opt] = rss_v[:, quarter(opt)]

    lax.fori_loop(0, chips // 2, outer_pair, 0)

    wait_bytes(bx_v.at[pl.ds(0, opts - 1)], recv_sem.at[18])
    part = bx_v[0].astype(F32)
    for k in range(1, opts):
        part = part + bx_v[k].astype(F32)
    by_v[...] = part.astype(BF16)
    for k in far_first:
        remote(by_v.at[k], bz_v.at[k], send_sem.at[19], recv_sem.at[19], yz(k)[1]).start()
    bz_v[0] = by_v[0]
    lax.fori_loop(chips // 2, chips, outer_pair, 0)

    wait_bytes(rsr_v.at[pl.ds(0, chips - 1)], recv_sem.at[10])
    acc = rsr_v[0].astype(F32)
    for k in range(1, chips):
        acc = acc + rsr_v[k].astype(F32)
    xg_v[opt] = acc.astype(BF16)
    for k in range(1, opts):
        same(xg_v.at[opt], send_sem.at[11], recv_sem.at[11], xp(k)[1]).start()

    wait_bytes(bz_v.at[pl.ds(0, chips - 1)], recv_sem.at[19])
    acc = bz_v[0].astype(F32)
    for k in range(1, chips):
        acc = acc + bz_v[k].astype(F32)
    bw_v[opt] = acc
    for k in range(1, opts):
        same(bw_v.at[opt], send_sem.at[20], recv_sem.at[20], xp(k)[1]).start()

    wait_bytes(mc_v.at[pl.ds(0, opts - 1)], recv_sem.at[14])
    wait_bytes(xg_v.at[pl.ds(0, opts - 1)], recv_sem.at[11])
    acc = xg_v[0].astype(F32)
    for k in range(1, opts):
        acc = acc + xg_v[k].astype(F32)
    wait_bytes(bw_v.at[pl.ds(0, opts - 1)], recv_sem.at[20])
    grad = jnp.transpose(jnp.concatenate([acc] + [bw_v[k] for k in range(opts)], axis=0))
    gt_v[...] = grad

    def over_all(buf, row, base, combine_fn):
        buf[seq, 0:1] = row
        for k in range(1, seqs):
            same(buf.at[seq, 0:1], send_sem.at[base], recv_sem.at[base], ((seq + k) % seqs, opt)).start()
        wait_bytes(buf.at[pl.ds(0, seqs - 1), 0:1], recv_sem.at[base])
        value = buf[0, 0:1]
        for k in range(1, seqs):
            value = combine_fn(value, buf[k, 0:1])
        return value

    col_raw = over_all(s_v, jnp.sum(grad * grad, axis=0, keepdims=True), 16, jnp.add)
    raw_total = jnp.sum(col_raw, axis=1, keepdims=True)
    factor = jnp.minimum(1.0, clip_norm / jnp.sqrt(raw_total + norm_floor))

    def moment_of(code, part):
        return beta_one * code.astype(F32) * mscale_ref[...] + (1.0 - beta_one) * (part * factor)

    top = jnp.zeros((1, 2 * N), F32)
    for k in range(opts):
        part = moment_of(mc_v[k], gt_v[k * rows : (k + 1) * rows])
        top = jnp.maximum(top, jnp.max(jnp.abs(part), axis=0, keepdims=True))
    peak = over_all(m_v, top, 17, jnp.maximum)

    own = gt_v[pl.ds(pl.multiple_of(opt * rows, rows), rows), :]
    scaled = own * factor
    moment = moment_of(mc_v[opt], own)
    squares = scaled * scaled
    old_total = jnp.sum(dc_v[:, 1, 0:1], axis=0, keepdims=True)
    col_next = beta_two * colstat_ref[...] + (1.0 - beta_two) * (factor * factor * col_raw / dim + tiny_square)
    eye = lax.broadcasted_iota(jnp.int32, (rows, rows), 0) == lax.broadcasted_iota(jnp.int32, (rows, rows), 1)
    old_col = jnp.sum(jnp.where(eye, jnp.broadcast_to(old_row, (rows, rows)), 0.0), axis=1, keepdims=True)
    row_next = beta_two * old_col + (1.0 - beta_two) * (
        jnp.sum(squares, axis=1, keepdims=True) / (2 * N) + tiny_square
    )
    row_mean = (
        beta_two * old_total + (1.0 - beta_two) * (factor * factor * raw_total / (2 * N) + dim * tiny_square)
    ) / dim
    second = row_next * col_next / row_mean
    upd_ref[...] = moment / (jnp.sqrt(second) + adam_floor) + weight_decay * w_ref[...]
    scale_next = peak + peak_floor
    scaleo_ref[...] = scale_next
    codeo_ref[...] = (moment / scale_next).astype(BF16)
    colo_ref[...] = col_next
    rowo_ref[...] = jnp.sum(jnp.where(eye, jnp.broadcast_to(row_next, (rows, rows)), 0.0), axis=0, keepdims=True)

    wait_bytes(wl_v.at[0, 0, pl.ds(0, opts - 1)], send_sem.at[0])
    wait_bytes(dlo_v, send_sem.at[1])
    wait_bytes(wl_v.at[pl.ds(0, chips - 1), 0, :], send_sem.at[2])
    wait_bytes(wl_v, send_sem.at[3])
    wait_bytes(dc_v.at[pl.ds(0, chips - 1)], send_sem.at[4])
    wait_bytes(pt_v, send_sem.at[5])
    wait_bytes(cb_v.at[:, pl.ds(0, chips - 1)], send_sem.at[6])
    wait_bytes(ob_v.at[:, pl.ds(0, chips - 1)], send_sem.at[7])
    wait_bytes(xb_v, send_sem.at[8])
    wait_bytes(rd_v, send_sem.at[9])
    wait_bytes(rsr_v.at[pl.ds(0, chips - 1)], send_sem.at[10])
    wait_bytes(xg_v.at[pl.ds(0, opts - 1)], send_sem.at[11])
    wait_bytes(wr_v.at[pl.ds(0, chips - 1), 0, 0], send_sem.at[12])
    wait_bytes(rx_v.at[pl.ds(0, opts - 1)], send_sem.at[13])
    wait_bytes(mc_v.at[pl.ds(0, opts - 1)], send_sem.at[14])
    wait_bytes(wr_v.at[:, 0, pl.ds(0, opts - 1)], send_sem.at[15])
    wait_bytes(bx_v.at[pl.ds(0, opts - 1)], send_sem.at[18])
    wait_bytes(by_v.at[pl.ds(0, chips - 1)], send_sem.at[19])
    wait_bytes(bw_v.at[pl.ds(0, opts - 1)], send_sem.at[20])
    for base, buf in ((16, s_v), (17, m_v)):
        wait_bytes(buf.at[pl.ds(0, seqs - 1), 0:1], send_sem.at[base])


def copy_out(*refs):
    sem = refs[-1]
    copies = []
    gi_ref, gi_out = refs[0], refs[6]
    pieces = 4
    size = gi_ref.shape[0] // pieces
    for k in range(pieces):
        at = pl.ds(k * size, size)
        copies.append(pltpu.make_async_copy(gi_ref.at[at], gi_out.at[at], sem.at[k]))
    for k in range(1, 6):
        copies.append(pltpu.make_async_copy(refs[k], refs[6 + k], sem.at[pieces + k - 1]))
    for copy in copies:
        copy.start()
    for copy in copies:
        copy.wait()


def per_device(
    seqs, opts, layer_in, ssm_input, grad_out, log_decay, skip_gain, w_bc, m_code, m_scale, row_stat, col_stat
):
    heads = skip_gain.shape[0]
    tokens, width = ssm_input.shape[1:]
    dim = layer_in.shape[2]
    rows = w_bc.shape[0]
    chips = seqs // 2
    rblk = rows * opts
    vm = pl.BlockSpec(memory_space=pltpu.VMEM)
    hbm = pl.BlockSpec(memory_space=pl.ANY)
    state = (2, chips, N, N)
    main = 2 * N * 3 // 4
    share = (2 * N - main) // opts
    scratch = [
        pltpu.VMEM((tokens, width), BF16),
        pltpu.VMEM((tokens, width), BF16),
        pltpu.VMEM((tokens, dim), BF16),
        pltpu.VMEM((tokens, width), BF16),
        pltpu.VMEM((tokens, width), BF16),
        pltpu.VMEM((chips, 2, opts, rows, N), BF16),
        pltpu.VMEM((chips, 2, opts, rows, N), BF16),
        pltpu.VMEM((N, tokens), F32),
        pltpu.VMEM((1, heads), F32),
        pltpu.VMEM((rows, 2 * N), F32),
        pltpu.VMEM((1, 2 * N), F32),
        pltpu.VMEM((1, rows), F32),
        pltpu.VMEM((1, 2 * N), F32),
        pltpu.VMEM((2, N, BLOCK), F32),
        pltpu.VMEM((tokens, N), F32),
        pltpu.VMEM((2, 8, width), F32),
        pltpu.VMEM((2, BLOCK, BLOCK), F32),
        pltpu.VMEM((2, BLOCK, BLOCK), F32),
        pltpu.VMEM((tokens, 2 * N), BF16),
        pltpu.VMEM((2 * N, tokens), BF16),
        pltpu.VMEM((N, width), F32),
        pltpu.VMEM((N, width), F32),
        pltpu.VMEM((2, 2, chips, N, N), BF16),
        pltpu.VMEM(state, BF16),
        pltpu.VMEM(state, BF16),
        pltpu.VMEM(state, BF16),
        pltpu.VMEM(state, BF16),
        pltpu.VMEM(state, BF16),
        pltpu.VMEM(state, BF16),
        pltpu.VMEM((2, 2, chips, N, N), BF16),
        pltpu.VMEM((2 * N, tokens), F32),
        pltpu.VMEM((2, chips, 2 * N, rblk), BF16),
        pltpu.VMEM((chips, 2 * N, rblk), BF16),
        pltpu.VMEM((chips, 2 * N, rblk), BF16),
        pltpu.VMEM((chips, main, rblk), BF16),
        pltpu.VMEM((opts, chips, share, rblk), BF16),
        pltpu.VMEM((chips, share, rblk), BF16),
        pltpu.VMEM((chips, share, rblk), BF16),
        pltpu.VMEM((opts, share, rblk), F32),
        pltpu.VMEM((opts, main, rblk), BF16),
        pltpu.VMEM((rblk, 2 * N), F32),
        pltpu.VMEM((opts, rows, 2 * N), BF16),
        pltpu.VMEM((opts, 8, N), F32),
        pltpu.VMEM((8, N), F32),
        pltpu.VMEM((8, N), F32),
        pltpu.VMEM((chips, 8, N), F32),
        pltpu.VMEM((seqs, 8, 2 * N), F32),
        pltpu.VMEM((seqs, 8, 2 * N), F32),
        pltpu.SemaphoreType.DMA((9,)),
        pltpu.SemaphoreType.DMA((7,)),
        pltpu.SemaphoreType.DMA((21,)),
        pltpu.SemaphoreType.DMA((21,)),
        pltpu.SemaphoreType.DMA((chips,)),
        pltpu.SemaphoreType.DMA((opts,)),
        pltpu.SemaphoreType.DMA((2, chips)),
        pltpu.SemaphoreType.DMA((2, 4)),
        pltpu.SemaphoreType.DMA((2, min(8, chips))),
        pltpu.SemaphoreType.DMA((min(8, chips),)),
    ]
    shapes = (
        jax.ShapeDtypeStruct((tokens, width), BF16),
        jax.ShapeDtypeStruct((rows, 2 * N), F32),
        jax.ShapeDtypeStruct((rows, 2 * N), BF16),
        jax.ShapeDtypeStruct((1, 2 * N), F32),
        jax.ShapeDtypeStruct((1, rows), F32),
        jax.ShapeDtypeStruct((1, 2 * N), F32),
    )
    out = pl.pallas_call(
        functools.partial(kernel, seqs, opts),
        out_shape=tuple(pltpu.VMEM(a.shape, a.dtype) for a in shapes),
        in_specs=[hbm] * 10,
        out_specs=(vm, vm, vm, vm, vm, vm),
        scratch_shapes=scratch,
        compiler_params=pltpu.CompilerParams(
            collective_id=0, has_side_effects=True, vmem_limit_bytes=60_000_000
        ),
    )(
        ssm_input[0],
        grad_out[0],
        layer_in[0],
        log_decay[0],
        skip_gain.reshape(1, heads),
        w_bc,
        m_code,
        m_scale.reshape(1, 2 * N),
        row_stat.reshape(1, rows),
        col_stat.reshape(1, 2 * N),
    )
    grad_input, update, code_next, scale_next, row_next, col_next = pl.pallas_call(
        copy_out,
        out_shape=shapes,
        in_specs=[vm] * 6,
        out_specs=(hbm,) * 6,
        scratch_shapes=[pltpu.SemaphoreType.DMA((9,))],
        compiler_params=pltpu.CompilerParams(vmem_limit_bytes=4_000_000),
    )(*[pltpu.with_memory_space_constraint(a, pltpu.VMEM) for a in out])
    return (
        grad_input[None],
        update,
        code_next,
        scale_next.reshape(2 * N),
        row_next.reshape(rows),
        col_next.reshape(2 * N),
    )


def solution(mesh):
    both = ("seq", "opt")
    return jax.shard_map(
        functools.partial(per_device, mesh.shape["seq"], mesh.shape["opt"]),
        mesh=mesh,
        in_specs=(
            P("opt", "seq", None),
            P("opt", "seq", None),
            P("opt", "seq", None),
            P("opt", None, "seq"),
            P(),
            P(both, None),
            P(both, None),
            P(),
            P(both),
            P(),
        ),
        out_specs=(P("opt", "seq", None), P(both, None), P(both, None), P(), P(both), P()),
        check_vma=False,
    )
```

time: 102 us -> 90.2 us (0.88)
  Pallas kernels: 101 us -> 89.3 us
    pallas_call x2, Pallas kernels: 101 us -> 89.3 us  [the longest x1 87.2 us: per_device(): pl.pallas_call(functools.partial(kernel, seqs, opts), out_shape=tuple((pl...]
where the time goes in v3:
time: 90.2 us; the launch traced here: 90.1 us
  Pallas kernels  89.3 us (99%)
    pallas_call x1, Pallas kernels, per_device(): pl.pallas_call(functools.partial(kernel, seqs, opts), out_shape=tuple((pl...  87.2 us
    pallas_call x1, Pallas kernels, per_device(): pl.pallas_call(copy_out, out_shape=shapes, in_specs=[vm] * 6, out_specs=(...  2.1 us

profile of v3, /device:TPU:1, one launch (start us, length us, event | category | flops | bytes accessed | tf_op | source)
XLA Modules:
  0.0 90.1 jit_solution(11871120323636356382)
XLA Ops:
  0.6 87.2 %shard_map.145 = (bf16[512,4096]{1,0:T(8,128)(2,1)S(1)}, f32[32,256]{1,0:T(8,128)S(1)}, bf16[32,256]{1,0:T(8,128)(2,1)S(1)}, f32[1,256]{1,0:T(1,128)S(1)}, f32[1,32]{1,0:T(1,128)S(1)}, /*index=5*/f32[1,256]{1,0:T(1,128)S(1)}) custom-call(bf16[512,4096]{1,0:T(8,128)(2,1)} %bitcast.12, bf16[512,4096]{1,0:T(8,128)(2,1)} %bitcast.13, ...), custom_call_target="tpu_custom_call" | custom-call | tf_op jit(solution)/shard_map/pallas_call | solution.py:762
  87.8 2.1 %shard_map.146 = (bf16[512,4096]{1,0:T(8,128)(2,1)}, f32[32,256]{1,0:T(8,128)}, bf16[32,256]{1,0:T(8,128)(2,1)}, f32[1,256]{1,0:T(1,128)}, f32[1,32]{1,0:T(1,128)}, /*index=5*/f32[1,256]{1,0:T(1,128)}) custom-call(bf16[512,4096]{1,0:T(8,128)(2,1)S(1)} %get-tuple-element.18.refs_0_, f32[32,256]{1,0:T(8,128)S(1)} %get-tuple-element.19.refs_1_, ...), custom_call_target="tpu_custom_call" | custom-call | tf_op jit(solution)/shard_map/pallas_call | solution.py:783

commit v4 on v3

--- a/solution.py
+++ b/solution.py
@@ -70,6 +70,7 @@
     erow_v,
     mix_v,
     aff_v,
+    proj_v,
     bc_v,
     bct_v,
     f0_v,
@@ -83,6 +84,7 @@
     xb_v,
     fin_v,
     gbt_v,
+    gbt_b,
     wg_v,
     rd_v,
     rss_v,
@@ -179,12 +181,6 @@
 
     lay_copy = pltpu.make_async_copy(lay_hbm, lay_v, in_sem.at[2 * groups])
 
-    barrier = pltpu.get_barrier_semaphore()
-    for k in range(1, seqs):
-        pl.semaphore_signal(barrier, inc=1, device_id=((seq + k) % seqs, opt), device_id_type=MESH)
-    for k in range(1, opts):
-        pl.semaphore_signal(barrier, inc=1, device_id=xp(k)[1], device_id_type=MESH)
-
     def small(source, target, k):
         return pltpu.make_async_copy(source, target, small_sem.at[k])
 
@@ -197,17 +193,24 @@
         small(mscale_hbm, mscale_ref, 5),
         small(colstat_hbm, colstat_ref, 6),
     ]
+    barrier = pltpu.get_barrier_semaphore()
+    for k in reversed(range(1, chips)):
+        for who in range(2):
+            pl.semaphore_signal(barrier, inc=1, device_id=(owner_after(k) * 2 + who, opt), device_id_type=MESH)
+    pl.semaphore_signal(barrier, inc=1, device_id=partner, device_id_type=MESH)
+    for k in range(1, opts):
+        pl.semaphore_signal(barrier, inc=1, device_id=xp(k)[1], device_id_type=MESH)
     for copy in smalls:
         copy.start()
+    if heads < N:
+        logp_v[heads:, :] = jnp.zeros((N - heads, logp_v.shape[1]), F32)
+    for copy in smalls:
+        copy.wait()
     for g in range(groups):
         for copy in in_copies(g):
             copy.start()
     lay_copy.start()
-    if heads < N:
-        logp_v[heads:, :] = jnp.zeros((N - heads, logp_v.shape[1]), F32)
-
-    for copy in smalls:
-        copy.wait()
+
     wl_v[chip, core, opt] = w_ref[:, 0:N].astype(BF16)
     wr_v[chip, core, opt] = w_ref[:, N:].astype(BF16)
     old_row = rowstat_ref[...]
@@ -250,7 +253,7 @@
         bottom = jnp.exp(jnp.where(tri_b, rs[:, half:] - rt[half:], -jnp.inf))
         return top, bottom
 
-    def mix_pair(hp, carry):
+    def mix_pair(products, scales, hp, carry):
         adds = [[None, None], [None, None]]
         for j in range(2):
             h = hp * 2 + j
@@ -261,37 +264,45 @@
                 xb = x_v[at, lanes]
                 db = dy_v[at, lanes]
                 rt = col[b * BLOCK : (b + 1) * BLOCK]
-                rs = r_v[b, pl.ds(h, 1), :]
-                prod = dot_nt(xb, db)
-                top, bottom = decays(rt, rs)
-                top = top * prod[0:half]
-                bottom = bottom * prod[half:, half:]
-                adds[b][0] = top if j == 0 else adds[b][0] + top
-                adds[b][1] = bottom if j == 0 else adds[b][1] + bottom
-                closing = rt[BLOCK - 1 : BLOCK]
-                erow_v[b, :, lanes] = jnp.broadcast_to(jnp.exp(closing), (8, N))
-                xs_v[at, lanes] = (xb.astype(F32) * jnp.exp(closing - rt)).astype(BF16)
-                ds_v[at, lanes] = (db.astype(F32) * jnp.exp(rt)).astype(BF16)
-        for b in range(2):
-            mix_v[b, 0:half, :] += adds[b][0]
-            mix_v[b, half:, half:] += adds[b][1]
+                if products:
+                    prod = dot_nt(xb, db)
+                    top, bottom = decays(rt, r_v[b, pl.ds(h, 1), :])
+                    top = top * prod[0:half]
+                    bottom = bottom * prod[half:, half:]
+                    adds[b][0] = top if j == 0 else adds[b][0] + top
+                    adds[b][1] = bottom if j == 0 else adds[b][1] + bottom
+                if scales:
+                    closing = rt[BLOCK - 1 : BLOCK]
+                    erow_v[b, :, lanes] = jnp.broadcast_to(jnp.exp(closing), (8, N))
+                    xs_v[at, lanes] = (xb.astype(F32) * jnp.exp(closing - rt)).astype(BF16)
+                    ds_v[at, lanes] = (db.astype(F32) * jnp.exp(rt)).astype(BF16)
+        if products:
+            for b in range(2):
+                mix_v[b, 0:half, :] += adds[b][0]
+                mix_v[b, half:, half:] += adds[b][1]
         return carry
 
     pairs = heads // 2
 
-    def mix_group(first_pair, last_pair):
+    def mix_group(first_part, last_part, products=True):
+        first_pair, last_pair = (pairs * part // 16 for part in (first_part, last_part))
         for g in range(groups):
             if first_pair <= g * (pairs // groups) < last_pair:
                 for copy in in_copies(g):
                     copy.wait()
-        lax.fori_loop(first_pair, last_pair, mix_pair, 0)
-
-    cuts = (0, pairs // 8, pairs // 4, pairs * 3 // 8, pairs)
-    mix_group(cuts[0], cuts[1])
+        lax.fori_loop(first_pair, last_pair, functools.partial(mix_pair, products, True), 0)
+
+    def share_left(some):
+        for k in some:
+            block = wl_v.at[owner_before(k), core]
+            wait_bytes(block, blk_sem.at[k])
+            same(block, send_sem.at[3], recv_sem.at[3], partner).start()
+
+    mix_group(0, 2)
     wait_bytes(wl_v.at[0, 0, pl.ds(0, opts - 1)], recv_sem.at[0])
     for k in far_first:
-        same(wl_v.at[chip, core, :], send_sem.at[2], blk_sem.at[k], yz(k)[1]).start()
-    same(wl_v.at[chip, core, :], send_sem.at[3], recv_sem.at[3], partner).start()
+        same(wl_v.at[chip, core], send_sem.at[2], blk_sem.at[k], yz(k)[1]).start()
+    same(wl_v.at[chip, core], send_sem.at[3], recv_sem.at[3], partner).start()
     wait_bytes(rx_v.at[pl.ds(0, opts - 1)], recv_sem.at[13])
     old_sum = rx_v[0]
     for k in range(1, opts):
@@ -299,29 +310,38 @@
     dlo_v[...] = old_sum
     dlo_v[0:1, :] = rt_v[BLOCK - 1 : BLOCK, :] + rt_v[2 * BLOCK - 1 : 2 * BLOCK, :]
     remote(dlo_v, dlp_v, send_sem.at[1], recv_sem.at[1], partner).start()
-    mix_group(cuts[1], cuts[2])
+    mix_group(2, 3)
     wait_bytes(wr_v.at[pl.ds(0, chips - 1), 0, 0], recv_sem.at[12])
     for k in range(1, opts):
         same(wr_v.at[:, core, opt], send_sem.at[15], half_sem.at[k], xp(k)[1]).start()
     same(wr_v.at[:, core, opt], send_sem.at[3], recv_sem.at[3], partner).start()
-    mix_group(cuts[2], cuts[3])
+    mix_group(3, 5)
     wait_bytes(dlp_v, recv_sem.at[1])
     dc_v[chip] = dlo_v[...] + dlp_v[...]
     for k in far_first:
         same(dc_v.at[chip], send_sem.at[4], recv_sem.at[4], yz(k)[1]).start()
-    mix_group(cuts[3], cuts[4])
-    for k in range(1, chips):
-        block = wl_v.at[owner_before(k), core, :]
-        wait_bytes(block, blk_sem.at[k])
-        same(block, send_sem.at[3], recv_sem.at[3], partner).start()
+    mix_group(5, 9)
+    share_left(far_first[: chips // 2])
+    mix_group(9, 10)
+    mix_group(10, 13, products=False)
+    share_left(far_first[chips // 2 :])
+    mix_group(13, 16, products=False)
     for k in range(1, opts):
         block = wr_v.at[:, core, (opt + opts - k) % opts]
         wait_bytes(block, half_sem.at[k])
         same(block, send_sem.at[3], recv_sem.at[3], partner).start()
     lay_copy.wait()
+
+    def proj_half(who):
+        rows_in = jnp.concatenate(
+            [lay_v[:, pl.ds(pl.multiple_of((2 * o + who) * rblk, rblk), rblk)] for o in range(chips)], axis=1
+        )
+        weights = [ref[:, who].reshape(chips * rblk, N) for ref in (wl_v, wr_v)]
+        return dot_nn(rows_in, jnp.concatenate(weights, axis=1))
+
+    proj_v[...] = proj_half(core)
     wait_bytes(wl_v, recv_sem.at[3])
-
-    proj = dot_nn(lay_v[...], jnp.concatenate([wl_v[...].reshape(dim, N), wr_v[...].reshape(dim, N)], axis=1)).astype(BF16)
+    proj = (proj_v[...] + proj_half(1 - core)).astype(BF16)
     bc_v[...] = proj
     bct_v[...] = jnp.transpose(proj.astype(F32)).astype(BF16)
     for b in range(2):
@@ -424,6 +444,7 @@
         ib_v[way, 0] = ob_v[way, chip]
 
     lax.fori_loop(0, heads // 4, inner_pair, 0)
+    lax.fori_loop(pairs * 10 // 16, pairs, functools.partial(mix_pair, True, False), 0)
     wait_bytes(dc_v.at[pl.ds(0, chips - 1)], recv_sem.at[4])
     scan_chips(0)
     lax.fori_loop(heads // 4, heads // 2, inner_pair, 0)
@@ -492,49 +513,47 @@
         wait_bytes(xb_v.at[way, pl.ds(start, fine)], fin_sem.at[way, g])
         lax.fori_loop(start, start + fine, functools.partial(finish_pair, way), 0, unroll=True)
 
-    steps = [(way, g) for way in range(2) for g in range(fines)]
     behind = 3
-    for i, (way, g) in enumerate(steps):
+
+    def enter_group(way, g):
         start = piece(g, fine)
         at = pl.ds(start, fine)
         for k in reversed(range(max(1, start), start + fine)):
             wait_bytes(ib_v.at[way, k], entry_sem.at[way, k])
         lax.fori_loop(start, start + fine, functools.partial(entry, way), 0, unroll=True)
         remote(xb_v.at[way, at], fin_v.at[way, core, at], send_sem.at[8], fin_sem.at[way, g], partner).start()
-        if i >= behind:
-            finish_group(*steps[i - behind])
-    for i in range(max(0, len(steps) - behind), len(steps)):
-        finish_group(*steps[i])
-
-    gbt_b = gbt_v[...].astype(BF16)
-
-    def weight_pair(k, carry):
-        lanes = pl.ds(pl.multiple_of(owner_after(k) * 2 * rblk, 2 * rblk), 2 * rblk)
-        part = dot_nn(gbt_b, lay_v[:, lanes]).astype(BF16)
-        wg_v[0, k] = part[:, 0:rblk]
-        wg_v[1, k] = part[:, rblk:]
-        return carry
-
-    def chip_sum(k, carry):
-        rss_v[k] = (wg_v[core, k].astype(F32) + rd_v[k].astype(F32)).astype(BF16)
-        return carry
-
-    cols = 2 * N
-    main = cols * 3 // 4
-    share = (cols - main) // opts
+
+    main = 2 * N * 3 // 4
+    share = (2 * N - main) // opts
+    spans = (pl.ds(N, N), pl.ds(0, N))
+    direct = (pl.ds(N, main - N), pl.ds(0, N))
 
     def quarter(who):
         return pl.ds(pl.multiple_of(main + who * share, share), share)
 
-    def sum_group(g):
+    def weight_pair(part, k, carry):
+        lanes = pl.ds(pl.multiple_of(owner_after(k) * 2 * rblk, 2 * rblk), 2 * rblk)
+        grads = dot_nn(gbt_b[spans[part], :], lay_v[:, lanes]).astype(BF16)
+        wg_v[0, part, k] = grads[:, 0:rblk]
+        wg_v[1, part, k] = grads[:, rblk:]
+        return carry
+
+    def chip_sum(part, k, carry):
+        both = wg_v[core, part, k].astype(F32) + rd_v[part, k].astype(F32)
+        rss_v[k, spans[part], :] = both.astype(BF16)
+        return carry
+
+    def sum_group(part, g):
         start = piece(g, fine)
         at = pl.ds(start, fine)
-        wait_bytes(rd_v.at[at], rs_sem.at[g])
-        lax.fori_loop(start, start + fine, chip_sum, 0, unroll=True)
+        wait_bytes(rd_v.at[part, at], rs_sem.at[part, g])
+        lax.fori_loop(start, start + fine, functools.partial(chip_sum, part), 0, unroll=True)
+        rows_at = direct[part]
         for k in reversed(range(max(1, start), start + fine)):
-            top = pl.ds(0, main)
-            remote(rss_v.at[k, top], rsr_v.at[k], send_sem.at[10], recv_sem.at[10], yz(k)[1]).start()
-        if (g + 1) * 2 % fines == 0:
+            remote(
+                rss_v.at[k, rows_at], rsr_v.at[k, rows_at], send_sem.at[10], recv_sem.at[21 if part == 0 else 10], yz(k)[1]
+            ).start()
+        if part == 0 and (g + 1) * 2 % fines == 0:
             half_at = pl.ds(start, chips // 2)
             for k in range(1, opts):
                 other, dev = xp(k)
@@ -542,39 +561,60 @@
                     rss_v.at[half_at, quarter(other)], bx_v.at[opt, half_at], send_sem.at[18], recv_sem.at[18], dev
                 ).start()
 
-    lag = 2
-    for g in range(fines):
+    def weight_group(part, g):
         start = piece(g, fine)
         at = pl.ds(start, fine)
-        lax.fori_loop(start, start + fine, weight_pair, 0, unroll=True)
-        remote(wg_v.at[1 - core, at], rd_v.at[at], send_sem.at[9], rs_sem.at[g], partner).start()
-        if g >= lag:
-            sum_group(g - lag)
-    for g in range(max(0, fines - lag), fines):
-        sum_group(g)
-    rsr_v[0] = rss_v[0, 0:main]
+        lax.fori_loop(start, start + fine, functools.partial(weight_pair, part), 0, unroll=True)
+        remote(
+            wg_v.at[1 - core, part, at], rd_v.at[part, at], send_sem.at[9], rs_sem.at[part, g], partner
+        ).start()
+
+    def arrived(part, sem):
+        rows_at = direct[part]
+        wait_bytes(rsr_v.at[pl.ds(0, chips - 1), rows_at], recv_sem.at[sem])
+        acc = rsr_v[0, rows_at, :].astype(F32)
+        for k in range(1, chips):
+            acc = acc + rsr_v[k, rows_at, :].astype(F32)
+        xg_v[opt, rows_at, :] = acc.astype(BF16)
+        for k in range(1, opts):
+            same(xg_v.at[opt, rows_at], send_sem.at[11], recv_sem.at[22 if part == 0 else 11], xp(k)[1]).start()
+
+    for i in range(fines + behind):
+        if i < fines:
+            enter_group(0, i)
+        if i >= behind:
+            finish_group(0, i - behind)
+    gbt_b[spans[0], :] = gbt_v[spans[0], :].astype(BF16)
+    for i in range(fines + behind):
+        for w in range(2 * i, min(2 * i + 2, fines)):
+            weight_group(0, w)
+        if i < fines:
+            enter_group(1, i)
+        for w in range(max(0, 2 * i - 4), min(2 * i - 2, fines)):
+            sum_group(0, w)
+        if i >= behind:
+            finish_group(1, i - behind)
+    rsr_v[0, direct[0], :] = rss_v[0, direct[0], :]
     bx_v[opt] = rss_v[:, quarter(opt)]
-
-    lax.fori_loop(0, chips // 2, outer_pair, 0)
-
+    gbt_b[spans[1], :] = gbt_v[spans[1], :].astype(BF16)
+    for i in range(fines):
+        weight_group(1, i)
+        if i >= behind:
+            sum_group(1, i - behind)
     wait_bytes(bx_v.at[pl.ds(0, opts - 1)], recv_sem.at[18])
-    part = bx_v[0].astype(F32)
+    part_x = bx_v[0].astype(F32)
     for k in range(1, opts):
-        part = part + bx_v[k].astype(F32)
-    by_v[...] = part.astype(BF16)
+        part_x = part_x + bx_v[k].astype(F32)
+    by_v[...] = part_x.astype(BF16)
     for k in far_first:
         remote(by_v.at[k], bz_v.at[k], send_sem.at[19], recv_sem.at[19], yz(k)[1]).start()
     bz_v[0] = by_v[0]
-    lax.fori_loop(chips // 2, chips, outer_pair, 0)
-
-    wait_bytes(rsr_v.at[pl.ds(0, chips - 1)], recv_sem.at[10])
-    acc = rsr_v[0].astype(F32)
-    for k in range(1, chips):
-        acc = acc + rsr_v[k].astype(F32)
-    xg_v[opt] = acc.astype(BF16)
-    for k in range(1, opts):
-        same(xg_v.at[opt], send_sem.at[11], recv_sem.at[11], xp(k)[1]).start()
-
+    for i in range(max(0, fines - behind), fines):
+        sum_group(1, i)
+    rsr_v[0, direct[1], :] = rss_v[0, direct[1], :]
+    arrived(0, 21)
+
+    lax.fori_loop(0, chips * 10 // 16, outer_pair, 0)
     wait_bytes(bz_v.at[pl.ds(0, chips - 1)], recv_sem.at[19])
     acc = bz_v[0].astype(F32)
     for k in range(1, chips):
@@ -582,9 +622,12 @@
     bw_v[opt] = acc
     for k in range(1, opts):
         same(bw_v.at[opt], send_sem.at[20], recv_sem.at[20], xp(k)[1]).start()
+    arrived(1, 10)
+    lax.fori_loop(chips * 10 // 16, chips, outer_pair, 0)
 
     wait_bytes(mc_v.at[pl.ds(0, opts - 1)], recv_sem.at[14])
-    wait_bytes(xg_v.at[pl.ds(0, opts - 1)], recv_sem.at[11])
+    for sem, rows_at in ((22, direct[0]), (11, direct[1])):
+        wait_bytes(xg_v.at[pl.ds(0, opts - 1), rows_at], recv_sem.at[sem])
     acc = xg_v[0].astype(F32)
     for k in range(1, opts):
         acc = acc + xg_v[k].astype(F32)
@@ -710,6 +753,7 @@
         pltpu.VMEM((2, 8, width), F32),
         pltpu.VMEM((2, BLOCK, BLOCK), F32),
         pltpu.VMEM((2, BLOCK, BLOCK), F32),
+        pltpu.VMEM((tokens, 2 * N), F32),
         pltpu.VMEM((tokens, 2 * N), BF16),
         pltpu.VMEM((2 * N, tokens), BF16),
         pltpu.VMEM((N, width), F32),
@@ -723,8 +767,9 @@
         pltpu.VMEM(state, BF16),
         pltpu.VMEM((2, 2, chips, N, N), BF16),
         pltpu.VMEM((2 * N, tokens), F32),
-        pltpu.VMEM((2, chips, 2 * N, rblk), BF16),
-        pltpu.VMEM((chips, 2 * N, rblk), BF16),
+        pltpu.VMEM((2 * N, tokens), BF16),
+        pltpu.VMEM((2, 2, chips, N, rblk), BF16),
+        pltpu.VMEM((2, chips, N, rblk), BF16),
         pltpu.VMEM((chips, 2 * N, rblk), BF16),
         pltpu.VMEM((chips, main, rblk), BF16),
         pltpu.VMEM((opts, chips, share, rblk), BF16),
@@ -742,14 +787,14 @@
         pltpu.VMEM((seqs, 8, 2 * N), F32),
         pltpu.SemaphoreType.DMA((9,)),
         pltpu.SemaphoreType.DMA((7,)),
-        pltpu.SemaphoreType.DMA((21,)),
-        pltpu.SemaphoreType.DMA((21,)),
+        pltpu.SemaphoreType.DMA((23,)),
+        pltpu.SemaphoreType.DMA((23,)),
         pltpu.SemaphoreType.DMA((chips,)),
         pltpu.SemaphoreType.DMA((opts,)),
         pltpu.SemaphoreType.DMA((2, chips)),
         pltpu.SemaphoreType.DMA((2, 4)),
         pltpu.SemaphoreType.DMA((2, min(8, chips))),
-        pltpu.SemaphoreType.DMA((min(8, chips),)),
+        pltpu.SemaphoreType.DMA((2, min(8, chips))),
     ]
     shapes = (
         jax.ShapeDtypeStruct((tokens, width), BF16),

time: 90.2 us -> 87.6 us (0.971)
  Pallas kernels: 89.3 us -> 86.6 us
    pallas_call x1, Pallas kernels: 87.2 us -> 84.5 us  [per_device(): pl.pallas_call(functools.partial(kernel, seqs, opts), out_shape=tuple((pl...]
where the time goes in v4:
time: 87.6 us; the launch traced here: 87.4 us
  Pallas kernels  86.6 us (99%)
    pallas_call x1, Pallas kernels, per_device(): pl.pallas_call(functools.partial(kernel, seqs, opts), out_shape=tuple((pl...  84.5 us
    pallas_call x1, Pallas kernels, per_device(): pl.pallas_call(copy_out, out_shape=shapes, in_specs=[vm] * 6, out_specs=(...  2.1 us

profile of v4, /device:TPU:1, one launch (start us, length us, event | category | flops | bytes accessed | tf_op | source)
XLA Modules:
  0.0 87.4 jit_solution(1655592107017430573)
XLA Ops:
  0.6 84.5 %shard_map.145 = (bf16[512,4096]{1,0:T(8,128)(2,1)S(1)}, f32[32,256]{1,0:T(8,128)S(1)}, bf16[32,256]{1,0:T(8,128)(2,1)S(1)}, f32[1,256]{1,0:T(1,128)S(1)}, f32[1,32]{1,0:T(1,128)S(1)}, /*index=5*/f32[1,256]{1,0:T(1,128)S(1)}) custom-call(bf16[512,4096]{1,0:T(8,128)(2,1)} %bitcast.12, bf16[512,4096]{1,0:T(8,128)(2,1)} %bitcast.13, ...), custom_call_target="tpu_custom_call" | custom-call | tf_op jit(solution)/shard_map/pallas_call | solution.py:807
  85.2 2.1 %shard_map.146 = (bf16[512,4096]{1,0:T(8,128)(2,1)}, f32[32,256]{1,0:T(8,128)}, bf16[32,256]{1,0:T(8,128)(2,1)}, f32[1,256]{1,0:T(1,128)}, f32[1,32]{1,0:T(1,128)}, /*index=5*/f32[1,256]{1,0:T(1,128)}) custom-call(bf16[512,4096]{1,0:T(8,128)(2,1)S(1)} %get-tuple-element.18.refs_0_, f32[32,256]{1,0:T(8,128)S(1)} %get-tuple-element.19.refs_1_, ...), custom_call_target="tpu_custom_call" | custom-call | tf_op jit(solution)/shard_map/pallas_call | solution.py:828

commit v5 on v4

--- a/solution.py
+++ b/solution.py
@@ -388,13 +388,18 @@
     def piece(g, size):
         return chips - (g + 1) * size
 
+    def to_owner(way, k):
+        sem = send_sem.at[6 if way == 0 else 21]
+        return remote(cb_v.at[way, k], rb_v.at[way, chip], sem, recv_sem.at[6 + way], yz(k)[1])
+
     def combine_group(way, g):
         start = piece(g, per)
         at = pl.ds(start, per)
         wait_bytes(pt_v.at[way, at], d2d_sem.at[way, g])
         lax.fori_loop(start, start + per, functools.partial(combine, way), 0, unroll=True)
-        for k in reversed(range(max(1, start), start + per)):
-            remote(cb_v.at[way, k], rb_v.at[way, chip], send_sem.at[6], recv_sem.at[6 + way], yz(k)[1]).start()
+        if way == 0:
+            for k in reversed(range(max(1, start), start + per)):
+                to_owner(way, k).start()
 
     steps = [(way, g) for way in range(2) for g in range(parts)]
     for i, (way, g) in enumerate(steps):
@@ -443,7 +448,11 @@
             remote(ob_v.at[way, other], ib_v.at[way, k], send_sem.at[7], entry_sem.at[way, k], dev).start()
         ib_v[way, 0] = ob_v[way, chip]
 
-    lax.fori_loop(0, heads // 4, inner_pair, 0)
+    lax.fori_loop(0, heads // 16, inner_pair, 0)
+    wait_bytes(cb_v.at[0, pl.ds(0, chips - 1)], send_sem.at[6])
+    for k in far_first:
+        to_owner(1, k).start()
+    lax.fori_loop(heads // 16, heads // 4, inner_pair, 0)
     lax.fori_loop(pairs * 10 // 16, pairs, functools.partial(mix_pair, True, False), 0)
     wait_bytes(dc_v.at[pl.ds(0, chips - 1)], recv_sem.at[4])
     scan_chips(0)
@@ -637,8 +646,11 @@
 
     def over_all(buf, row, base, combine_fn):
         buf[seq, 0:1] = row
-        for k in range(1, seqs):
-            same(buf.at[seq, 0:1], send_sem.at[base], recv_sem.at[base], ((seq + k) % seqs, opt)).start()
+        for e in far_first:
+            there = owner_after(e) * 2
+            for who in range(2):
+                same(buf.at[seq, 0:1], send_sem.at[base], recv_sem.at[base], (there + who, opt)).start()
+        same(buf.at[seq, 0:1], send_sem.at[base], recv_sem.at[base], partner).start()
         wait_bytes(buf.at[pl.ds(0, seqs - 1), 0:1], recv_sem.at[base])
         value = buf[0, 0:1]
         for k in range(1, seqs):
@@ -686,7 +698,7 @@
     wait_bytes(wl_v, send_sem.at[3])
     wait_bytes(dc_v.at[pl.ds(0, chips - 1)], send_sem.at[4])
     wait_bytes(pt_v, send_sem.at[5])
-    wait_bytes(cb_v.at[:, pl.ds(0, chips - 1)], send_sem.at[6])
+    wait_bytes(cb_v.at[1, pl.ds(0, chips - 1)], send_sem.at[21])
     wait_bytes(ob_v.at[:, pl.ds(0, chips - 1)], send_sem.at[7])
     wait_bytes(xb_v, send_sem.at[8])
     wait_bytes(rd_v, send_sem.at[9])

time: 87.6 us -> 87.6 us (level)
  no operation moved by 1% of the time
where the time goes in v5:
time: 87.6 us; the launch traced here: 87.4 us
  Pallas kernels  86.6 us (99%)
    pallas_call x1, Pallas kernels, per_device(): pl.pallas_call(functools.partial(kernel, seqs, opts), out_shape=tuple((pl...  84.5 us
    pallas_call x1, Pallas kernels, per_device(): pl.pallas_call(copy_out, out_shape=shapes, in_specs=[vm] * 6, out_specs=(...  2.1 us

profile of v5, /device:TPU:1, one launch (start us, length us, event | category | flops | bytes accessed | tf_op | source)
XLA Modules:
  0.0 87.4 jit_solution(15636569828739450925)
XLA Ops:
  0.6 84.5 %shard_map.145 = (bf16[512,4096]{1,0:T(8,128)(2,1)S(1)}, f32[32,256]{1,0:T(8,128)S(1)}, bf16[32,256]{1,0:T(8,128)(2,1)S(1)}, f32[1,256]{1,0:T(1,128)S(1)}, f32[1,32]{1,0:T(1,128)S(1)}, /*index=5*/f32[1,256]{1,0:T(1,128)S(1)}) custom-call(bf16[512,4096]{1,0:T(8,128)(2,1)} %bitcast.12, bf16[512,4096]{1,0:T(8,128)(2,1)} %bitcast.13, ...), custom_call_target="tpu_custom_call" | custom-call | tf_op jit(solution)/shard_map/pallas_call | solution.py:819
  85.1 2.1 %shard_map.146 = (bf16[512,4096]{1,0:T(8,128)(2,1)}, f32[32,256]{1,0:T(8,128)}, bf16[32,256]{1,0:T(8,128)(2,1)}, f32[1,256]{1,0:T(1,128)}, f32[1,32]{1,0:T(1,128)}, /*index=5*/f32[1,256]{1,0:T(1,128)}) custom-call(bf16[512,4096]{1,0:T(8,128)(2,1)S(1)} %get-tuple-element.18.refs_0_, f32[32,256]{1,0:T(8,128)S(1)} %get-tuple-element.19.refs_1_, ...), custom_call_target="tpu_custom_call" | custom-call | tf_op jit(solution)/shard_map/pallas_call | solution.py:840
